TPU v7x, 32 devices: a whole 2x2x4 slice. The times are simulated.
32 devices in a mesh: zone: 8 (over z, x), freq: 4 (over y, core).
Axes of the slice: x: 2, y: 2, z: 4, core: 2. Of those that a mesh axis runs over, the one named last changes fastest.
Arguments:
- modulus: float32 [64, 3, 1, 1024], P('zone'), may hold values from 0.3 to 1.5
- first_moment: float32 [64, 3, 1, 1024], P('zone'), may hold values from -6 to 6
- second_moment: float32 [64, 3, 1, 1024], P('zone'), may hold values from 0.5 to 4
- fiber: float32 [64, 1, 1024], P('zone'), may hold values from -1 to 1
- measured: float32 [4, 32, 2, 8, 1024], P('freq', 'zone'), may hold values from -6 to 6
- wave_sq: float32 [4], P('freq'), may hold values from 0.5 to 5
- send_list: int32 [8, 8, 2], P('zone'), may hold values from -1 to 7, as said below
- brick_list: int32 [32, 8], P('zone'), may hold values from 0 to 15, as said below
Outputs:
- new_modulus: float32 [64, 3, 1, 1024], P('zone')
- new_first: float32 [64, 3, 1, 1024], P('zone')
- new_second: float32 [64, 3, 1, 1024], P('zone')
Inputs may be any that keep to these rules, and one draw needn't show every extreme that they name: `send_list`: entries are -1 or distinct local brick indices; for each owner and zone group the live slots are c < some count of 0 to 2, and owner o sends 2 bricks to group (o + 1) % 8. `brick_list`: every entry names a live slot of its zone group.
All inputs are finite; a program needn't handle non-finite values.
Results may differ from a plain program's by a relative error of at most 0.0001.
Values sent between devices are 32-bit elements; how exact they have to be, the bound alone decides.
No kernel may reach another device: no remote copies, remote signals or barrier semaphores. Data moves between devices by JAX's collectives and lax.ppermute only.
A program may use at most 64 MiB of HBM per device.

v0:
```python
import jax
import jax.numpy as jnp
from jax import lax
from jax.sharding import PartitionSpec as P

BY = 32
BZ = 32
K = 8
SWEEPS = 6


relax_rate = 0.25
learn_rate = 0.1
beta_first = 0.9
beta_second = 0.99
smooth_rate = 0.5
adam_eps = 1e-08


def beside_sum(cube):
    padded = jnp.pad(cube, ((0, 0), (1, 1), (1, 1), (1, 1)))
    total = padded[:, 2:, 1:-1, 1:-1] + padded[:, :-2, 1:-1, 1:-1]
    total = total + padded[:, 1:-1, 2:, 1:-1] + padded[:, 1:-1, :-2, 1:-1]
    return total + padded[:, 1:-1, 1:-1, 2:] + padded[:, 1:-1, 1:-1, :-2]


def misfit(moduli, fiber_tile, observed, wave_value):
    shear = (moduli[0] + (moduli[1] - moduli[0]) * fiber_tile * fiber_tile).reshape(-1, BY, BZ)
    damping = moduli[2].reshape(-1, BY, BZ)
    diagonal_term = 6.0 * shear + wave_value
    start_field = observed.reshape(2, -1, BY, BZ)
    field = start_field
    for sweep_index in range(SWEEPS):
        stencil = 6.0 * field - beside_sum(field)
        resid_real = shear * (stencil[0] - damping * stencil[1]) - wave_value * field[0]
        resid_imag = shear * (stencil[1] + damping * stencil[0]) - wave_value * field[1]
        field = field - relax_rate * jnp.stack([resid_real, resid_imag]) / diagonal_term
    gap = field - start_field
    return jnp.sum(gap * gap)


def update(moduli, first_moment, second_moment, fiber_tile, descent):
    new_first = beta_first * first_moment + (1.0 - beta_first) * descent
    new_second = beta_second * second_moment + (1.0 - beta_second) * descent * descent
    stepped = moduli - learn_rate * new_first / (jnp.sqrt(new_second) + adam_eps)
    shaped = stepped.reshape(stepped.shape[:-1] + (-1, BZ))
    lower_cell = jnp.concatenate([shaped[..., :1], shaped[..., :-1]], axis=-1).reshape(
        stepped.shape
    )
    upper_cell = jnp.concatenate([shaped[..., 1:], shaped[..., -1:]], axis=-1).reshape(
        stepped.shape
    )
    weight = smooth_rate * (fiber_tile * fiber_tile)[:, None]
    smoothed = stepped + weight * (0.5 * (lower_cell + upper_cell) - stepped)
    return (smoothed, new_first, new_second)


def to_owned(returned, owner_pick):
    flattened = returned.reshape(owner_pick.shape[1], -1)
    return jnp.dot(owner_pick, flattened, precision=lax.Precision.HIGHEST)


def on_device(
    modulus, first_moment, second_moment, fiber, measured, wave_sq, send_list, brick_list
):
    zone_count = lax.axis_size("zone")
    freq_count = lax.axis_size("freq")
    owned_count = modulus.shape[0]
    rows_brick = modulus.shape[2]
    depth = modulus.shape[3]
    slot_cap = send_list.shape[2]
    owner_list = send_list[0]
    live_mask = owner_list >= 0
    safe_ids = jnp.where(live_mask, owner_list, 0)
    stacked = jnp.concatenate([modulus, fiber[:, None]], axis=1)
    outgoing = jnp.where(live_mask[:, :, None, None, None], stacked[safe_ids], 0.0)
    arrived = lax.all_to_all(outgoing, "zone", split_axis=0, concat_axis=0, tiled=True)
    slot_data = arrived.reshape(zone_count * slot_cap, 4, rows_brick, depth)
    wave_value = wave_sq[0]

    def solve(subzone_item):
        brick_ids, observed = subzone_item
        picked_rows = slot_data[brick_ids]
        subzone_par = jnp.swapaxes(picked_rows, 0, 1).reshape(4, K * rows_brick, depth)
        gradient = jax.grad(misfit)(subzone_par[:3], subzone_par[3], observed, wave_value)
        return jnp.swapaxes(gradient.reshape(3, K, rows_brick, depth), 0, 1)

    gradients = lax.map(solve, (brick_list, measured[0]))
    flattened = gradients.reshape(-1, 3 * rows_brick * depth)
    references = brick_list.reshape(-1)
    slot_iota = jnp.arange(zone_count * slot_cap, dtype=jnp.int32)
    selector = (references[None, :] == slot_iota[:, None]).astype(jnp.float32)
    slot_grad = jnp.dot(selector, flattened, precision=lax.Precision.HIGHEST)
    slot_grad = slot_grad.reshape(zone_count, slot_cap, 3, rows_brick, depth)
    use_count = jnp.sum(selector, axis=1).reshape(zone_count, slot_cap)
    owned_iota = jnp.arange(owned_count, dtype=jnp.int32)
    owner_pick = (owner_list.reshape(-1)[None, :] == owned_iota[:, None]).astype(jnp.float32)
    shares = lax.psum_scatter(slot_grad, "freq", scatter_dimension=4, tiled=True)
    share_cells = shares.shape[4]
    returned, returned_uses = (
        lax.all_to_all(shares, "zone", split_axis=0, concat_axis=0, tiled=True),
        lax.all_to_all(use_count, "zone", split_axis=0, concat_axis=0, tiled=True),
    )
    grad_total = to_owned(returned, owner_pick).reshape(owned_count, 3, rows_brick, share_cells)
    intersection = jnp.dot(owner_pick, returned_uses.reshape(-1), precision=lax.Precision.HIGHEST)
    descent = grad_total / (freq_count * jnp.maximum(intersection, 1.0))[:, None, None, None]
    cell_start = lax.axis_index("freq") * share_cells
    mod_share = lax.dynamic_slice_in_dim(modulus, cell_start, share_cells, 3)
    first_share = lax.dynamic_slice_in_dim(first_moment, cell_start, share_cells, 3)
    second_share = lax.dynamic_slice_in_dim(second_moment, cell_start, share_cells, 3)
    fiber_share = lax.dynamic_slice_in_dim(fiber, cell_start, share_cells, 2)
    smoothed, new_first, new_second = update(
        mod_share, first_share, second_share, fiber_share, descent
    )
    return (
        lax.all_gather(smoothed, "freq", axis=3, tiled=True),
        lax.all_gather(new_first, "freq", axis=3, tiled=True),
        lax.all_gather(new_second, "freq", axis=3, tiled=True),
    )


def solution(mesh):
    placed = (
        P("zone", None, None, None),
        P("zone", None, None, None),
        P("zone", None, None, None),
        P("zone", None, None),
        P("freq", "zone", None, None, None),
        P("freq"),
        P("zone", None, None),
        P("zone", None),
    )
    return jax.shard_map(
        on_device,
        mesh=mesh,
        in_specs=placed,
        out_specs=(
            P("zone", None, None, None),
            P("zone", None, None, None),
            P("zone", None, None, None),
        ),
        check_vma=False,
    )
```

profile of v0, /device:TPU:0, one launch (start us, length us, event | category | flops | bytes accessed | tf_op | source)
XLA Modules:
  0.0 273.9 jit_solution(16547523354455875704)
XLA Ops:
  10.8 7.3 %all-to-all-start = ((f32[8,2,4,1,1024]{4,2,1,3,0:T(4,128)}), f32[8,2,4,1,1024]{4,2,1,3,0:T(4,128)S(1)}, u32[]{:S(2)}, u32[]{:S(2)}) async-start(f32[8,2,4,1,1024]{4,2,1,3,0:T(4,128)} %broadcast_select_fusion), calls=%async_computation | async-start | bytes 524288 | tf_op jit(solution)/shard_map/all_to_all | solution.py:77
  18.9 8.1 %all-to-all-done = f32[8,2,4,1,1024]{4,2,1,3,0:T(4,128)S(1)} async-done(((f32[8,2,4,1,1024]{4,2,1,3,0:T(4,128)}), f32[8,2,4,1,1024]{4,2,1,3,0:T(4,128)S(1)}, u32[]{:S(2)}, u32[]{:S(2)}) %all-to-all-start) | async-done | bytes 262176 | tf_op jit(solution)/shard_map/all_to_all | solution.py:77
  27.0 186.4 %while.12 = (s32[]{:T(128)}, f32[4,8,3,1,1024]{4,1,2,3,0:T(8,128)}, s32[4,8]{1,0:T(4,128)S(1)}, f32[16,4,1,1024]{3,1,0,2:T(4,128)S(1)}, f32[4,2,8,1024]{3,2,1,0:...) while((s32[]{:T(128)}, f32[4,8,3,1,1024]{4,1,2,3,0:T(8,128)}, s32[4,8]{1,0:T(4,128)S(1)}, ...), condition=%wide.region_7.8_spmd, body=%wide.region_0.7_spmd.sunk | while | flops 7111707 | bytes 26416316 | solution.py:88
  27.1 1.5 dynamic-slice_multiply_fusion.3
  31.7 1.3 multiply_divide_fusion.4
  58.6 1.4 fusion.212
  62.7 1.5 fusion.214
  64.2 1.6 unstack.190
  73.7 1.5 dynamic-slice_multiply_fusion.3
  78.4 1.3 multiply_divide_fusion.4
  105.2 1.4 fusion.212
  109.3 1.5 fusion.214
  110.8 1.6 unstack.190
  120.3 1.5 dynamic-slice_multiply_fusion.3
  125.0 1.3 multiply_divide_fusion.4
  151.8 1.4 fusion.212
  155.9 1.5 fusion.214
  157.4 1.6 unstack.190
  166.9 1.5 dynamic-slice_multiply_fusion.3
  198.5 1.4 fusion.212
  202.5 1.5 fusion.214
  204.0 1.6 unstack.190
  213.5 2.0 convolution_bitcast_fusion
  216.2 3.6 %all-to-all-start.2 = ((f32[8,1,2]{2,1,0:T(1,128)}), f32[8,1,2]{2,1,0:T(1,128)S(1)}, u32[]{:S(2)}, u32[]{:S(2)}) async-start(f32[8,1,2]{2,1,0:T(1,128)} %bitcast.31), calls=%async_computation.3 | async-start | bytes 8192 | tf_op jit(solution)/shard_map/all_to_all | solution.py:102
  222.2 4.0 %all-to-all-done.2 = f32[8,1,2]{2,1,0:T(1,128)S(1)} async-done(((f32[8,1,2]{2,1,0:T(1,128)}), f32[8,1,2]{2,1,0:T(1,128)S(1)}, u32[]{:S(2)}, u32[]{:S(2)}) %all-to-all-start.2) | async-done | bytes 96 | tf_op jit(solution)/shard_map/all_to_all | solution.py:102
  227.5 6.9 %reduce-scatter.2.cloned.1.call-done = f32[8,2,3,1,256]{4,0,2,1,3:T(8,128)} async-done(((f32[8,2,3,1,1024]{4,0,2,1,3:T(8,128)}), f32[8,2,3,1,256]{4,0,2,1,3:T(8,128)}) %reduce-scatter.2.cloned.1.call-update) | async-done | bytes 49168 | tf_op jit(solution)/shard_map/reduce_scatter | solution.py:98
  234.4 1.4 copy.105
  235.9 5.5 %all-to-all-start.1 = ((f32[8,2,3,1,256]{4,1,3,2,0:T(2,128)}), f32[8,2,3,1,256]{4,1,3,2,0:T(2,128)S(1)}, u32[]{:S(2)}, u32[]{:S(2)}) async-start(f32[8,2,3,1,256]{4,1,3,2,0:T(2,128)} %copy.105), calls=%async_computation.2 | async-start | bytes 98304 | tf_op jit(solution)/shard_map/all_to_all | solution.py:101
  241.5 6.7 %all-to-all-done.1 = f32[8,2,3,1,256]{4,1,3,2,0:T(2,128)S(1)} async-done(((f32[8,2,3,1,256]{4,1,3,2,0:T(2,128)}), f32[8,2,3,1,256]{4,1,3,2,0:T(2,128)S(1)}, u32[]{:S(2)}, u32[]{:S(2)}) %all-to-all-start.1) | async-done | bytes 49184 | tf_op jit(solution)/shard_map/all_to_all | solution.py:101
  248.6 5.3 %all_gather.10 = f32[8,3,1,1024]{3,0,1,2:T(8,128)S(1)} all-gather(f32[8,3,1,256]{3,0,1,2:T(8,128)S(1)} %get-tuple-element.153), channel_id=1, replica_groups=mesh['zone'=8,'freq'=4] {'freq'}, dimensions={3}, use_global_device_ids=true | all-gather | bytes 122880 | tf_op jit(solution)/shard_map/all_gather | solution.py:117
  254.7 5.3 %all_gather.11 = f32[8,3,1,1024]{3,0,1,2:T(8,128)S(1)} all-gather(f32[8,3,1,256]{3,0,1,2:T(8,128)S(1)} %get-tuple-element.154), channel_id=1, replica_groups=mesh['zone'=8,'freq'=4] {'freq'}, dimensions={3}, use_global_device_ids=true | all-gather | bytes 122880 | tf_op jit(solution)/shard_map/all_gather | solution.py:118
  261.0 5.3 %all_gather.9 = f32[8,3,1,1024]{3,0,1,2:T(8,128)S(1)} all-gather(f32[8,3,1,256]{3,0,1,2:T(8,128)S(1)} %multiply_add_fusion.2), channel_id=1, replica_groups=mesh['zone'=8,'freq'=4] {'freq'}, dimensions={3}, use_global_device_ids=true | all-gather | bytes 122880 | tf_op jit(solution)/shard_map/all_gather | solution.py:116
  (715 shorter events, 168.0 us)
Async XLA Ops:
  10.8 16.2 %all-to-all-start = ((f32[8,2,4,1,1024]{4,2,1,3,0:T(4,128)}), f32[8,2,4,1,1024]{4,2,1,3,0:T(4,128)S(1)}, u32[]{:S(2)}, u32[]{:S(2)}) async-start(f32[8,2,4,1,1024]{4,2,1,3,0:T(4,128)} %broadcast_select_fusion), calls=%async_computation | async-start | bytes 524288 | tf_op jit(solution)/shard_map/all_to_all | solution.py:77
  18.1 216.3 %reduce-scatter.2.cloned.1.call-start = ((), (), s32[]{:S(2)}) async-start(), calls=%async_computation.4 | async-start | bytes 245760 | tf_op jit(solution)/shard_map/reduce_scatter | solution.py:98
  27.0 3.1 %copy-start.30 = (f32[16,4,1,1024]{3,1,0,2:T(4,128)}, f32[16,4,1,1024]{3,1,0,2:T(4,128)S(1)}, u32[]{:S(2)}) copy-start(f32[16,4,1,1024]{3,1,0,2:T(4,128)S(1)} %get-tuple-element.494) | copy-start | bytes 786436 | tf_op jit(solution)/shard_map/while
  30.4 1.1 copy-start.1
  61.5 0.9 copy-start.5
  66.5 0.9 copy-start.3
  66.5 1.0 copy-start.4
  67.5 1.0 copy-start.6
  69.3 1.0 copy-start
  72.7 1.0 copy-start.31
  73.6 3.1 %copy-start.30 = (f32[16,4,1,1024]{3,1,0,2:T(4,128)}, f32[16,4,1,1024]{3,1,0,2:T(4,128)S(1)}, u32[]{:S(2)}) copy-start(f32[16,4,1,1024]{3,1,0,2:T(4,128)S(1)} %get-tuple-element.494) | copy-start | bytes 786436 | tf_op jit(solution)/shard_map/while
  77.0 1.1 copy-start.1
  113.1 1.0 copy-start.4
  114.1 1.0 copy-start.6
  115.9 1.0 copy-start
  119.3 1.0 copy-start.31
  120.2 3.1 %copy-start.30 = (f32[16,4,1,1024]{3,1,0,2:T(4,128)}, f32[16,4,1,1024]{3,1,0,2:T(4,128)S(1)}, u32[]{:S(2)}) copy-start(f32[16,4,1,1024]{3,1,0,2:T(4,128)S(1)} %get-tuple-element.494) | copy-start | bytes 786436 | tf_op jit(solution)/shard_map/while
  123.6 1.1 copy-start.1
  154.7 0.9 copy-start.5
  159.7 0.9 copy-start.3
  159.7 1.0 copy-start.4
  160.7 1.0 copy-start.6
  162.6 1.0 copy-start
  165.9 1.0 copy-start.31
  166.9 3.1 %copy-start.30 = (f32[16,4,1,1024]{3,1,0,2:T(4,128)}, f32[16,4,1,1024]{3,1,0,2:T(4,128)S(1)}, u32[]{:S(2)}) copy-start(f32[16,4,1,1024]{3,1,0,2:T(4,128)S(1)} %get-tuple-element.494) | copy-start | bytes 786436 | tf_op jit(solution)/shard_map/while
  170.2 1.1 copy-start.1
  206.3 1.0 copy-start.4
  207.3 1.0 copy-start.6
  209.2 1.0 copy-start
  212.5 1.0 copy-start.31
  216.2 10.0 %all-to-all-start.2 = ((f32[8,1,2]{2,1,0:T(1,128)}), f32[8,1,2]{2,1,0:T(1,128)S(1)}, u32[]{:S(2)}, u32[]{:S(2)}) async-start(f32[8,1,2]{2,1,0:T(1,128)} %bitcast.31), calls=%async_computation.3 | async-start | bytes 8192 | tf_op jit(solution)/shard_map/all_to_all | solution.py:102
  235.9 12.3 %all-to-all-start.1 = ((f32[8,2,3,1,256]{4,1,3,2,0:T(2,128)}), f32[8,2,3,1,256]{4,1,3,2,0:T(2,128)S(1)}, u32[]{:S(2)}, u32[]{:S(2)}) async-start(f32[8,2,3,1,256]{4,1,3,2,0:T(2,128)} %copy.105), calls=%async_computation.2 | async-start | bytes 98304 | tf_op jit(solution)/shard_map/all_to_all | solution.py:101
  (102 other events, 85.2 us)
Sparse Core Ops, SparseCore 0:
  215.6 18.7 reduce-scatter.1
where the time goes:
time: 277 us; the launch traced here: 274 us
  local copies, waits for them, and re-layouts  112 us (40%)
  other arithmetic  85.3 us (31%)
  waiting for transfers between devices  25.8 us (9%)
  starting transfers between devices  16.4 us (6%)
  blocking collectives  16 us (6%)
  between operations  14.1 us (5%)
    another operation x100, local copies, waits for them, and re-layouts, misfit(): jnp.stack([resid_real, resid_imag])  38.5 us
    another operation x20, other arithmetic, misfit(): jnp.stack([resid_real, resid_imag])  20.5 us
    squeeze x24, local copies, waits for them, and re-layouts, misfit(): stencil[0] - damping * stencil[1]  17.4 us
    squeeze x24, local copies, waits for them, and re-layouts, misfit(): stencil[1]  17.3 us
    sub x24, other arithmetic, misfit(): shear * (stencil[0] - damping * stencil[1]) - wave_value * field[0]  14.6 us
    while x260, local copies, waits for them, and re-layouts  14.2 us
    mul x24, other arithmetic, misfit(): relax_rate * jnp.stack([resid_real, resid_imag]) / diagonal_term  10.9 us
    all_to_all x1, waiting for transfers between devices, on_device(): lax.all_to_all(outgoing, 'zone', split_axis=0, concat_axis=0, tiled=True)  8.15 us
  transfers between devices with their start and end apart: 4, of which 4 were waited for; matrix products, arithmetic and copies ran while one was open for 1% of the time, Pallas kernels for 0%

commit v1 on v0

v1 whole, which is shorter than its diff:
```python
import functools

import jax
import jax.numpy as jnp
from jax import lax
from jax.experimental import pallas as pl
from jax.experimental.pallas import tpu as pltpu
from jax.sharding import Mesh, PartitionSpec as P

BZ = 32
K = 8
SWEEPS = 6
LANES = 128
SUBL = 8

relax_rate = 0.25
learn_rate = 0.1
beta_first = 0.9
beta_second = 0.99
smooth_rate = 0.5
adam_eps = 1e-08

VMEM = pl.BlockSpec(memory_space=pltpu.VMEM)
SMEM = pl.BlockSpec(memory_space=pltpu.SMEM)


def pack_kernel(send_ref, brick_ref, modulus_ref, fiber_ref, out_ref, plane_ref):
    cap, zones = send_ref.shape
    owned = modulus_ref.shape[0]
    for b in range(owned):
        fib = fiber_ref[b]
        base = modulus_ref[b, 0]
        plane_ref[b, 0] = base + (modulus_ref[b, 1] - base) * fib * fib
        plane_ref[b, 1] = modulus_ref[b, 2]
    for d in range(zones):
        for c in range(cap):
            local = jnp.maximum(send_ref[c, d], 0)
            out_ref[d, c] = plane_ref[local]
    slot_at = lax.broadcasted_iota(jnp.int32, (SUBL, LANES), 1)
    for first in range(0, zones * cap, LANES):
        uses = jnp.zeros((SUBL, LANES), jnp.float32)
        for s in range(brick_ref.shape[0]):
            for k in range(brick_ref.shape[1]):
                uses = uses + jnp.where(slot_at == brick_ref[s, k] - first, 1.0, 0.0)
        for q in range(first, min(first + LANES, zones * cap)):
            wide = jnp.broadcast_to(uses[:, q - first : q - first + 1], (SUBL, LANES))
            out_ref[q // cap, cap + (q % cap) // 2, (q % cap) % 2] = wide


def solve_kernel(brick_ref, wave_ref, data_ref, seen_ref, out_ref, coef_ref, field_ref, sten_ref, lam_ref, grad_ref):
    subzones, entries = brick_ref.shape
    cap = out_ref.shape[2]
    wave = wave_ref[0]
    row = lax.broadcasted_iota(jnp.int32, (SUBL, LANES), 0)
    lane = lax.broadcasted_iota(jnp.int32, (SUBL, LANES), 1)
    z_first = lane % BZ == 0
    z_last = lane % BZ == BZ - 1
    low_lane = lane < BZ
    high_lane = lane >= LANES - BZ
    y_first = jnp.logical_and(row == 0, low_lane)
    y_last = jnp.logical_and(row == SUBL - 1, high_lane)

    def plane_sum(v):
        zm = jnp.where(z_first, 0.0, pltpu.roll(v, 1, 1))
        zp = jnp.where(z_last, 0.0, pltpu.roll(v, LANES - 1, 1))
        ym = pltpu.roll(v, BZ, 1)
        ym = jnp.where(low_lane, pltpu.roll(ym, 1, 0), ym)
        ym = jnp.where(y_first, 0.0, ym)
        yp = pltpu.roll(v, LANES - BZ, 1)
        yp = jnp.where(high_lane, pltpu.roll(yp, SUBL - 1, 0), yp)
        yp = jnp.where(y_last, 0.0, yp)
        return (zm + zp) + (ym + yp)

    def stencil(vs):
        sums = [plane_sum(v) for v in vs]
        res = []
        for x, v in enumerate(vs):
            total = sums[x]
            if x > 0:
                total = total + vs[x - 1]
            if x + 1 < len(vs):
                total = total + vs[x + 1]
            res.append(6.0 * v - total)
        return res

    for s in range(subzones):
        for k in range(entries):
            q = brick_ref[s, k]
            pair = data_ref[q // cap, q % cap]
            shear, damping = pair[0], pair[1]
            rate = relax_rate / (6.0 * shear + wave)
            beta = rate * shear
            coef_ref[s, 0, k] = 1.0 + rate * wave
            coef_ref[s, 1, k] = beta
            coef_ref[s, 2, k] = beta * damping
            for p in range(2):
                at = ((s * 2 + p) * SUBL) * K + k
                field_ref[0, s, p, k] = seen_ref[pl.ds(at, SUBL, stride=K), :]

    for t in range(SWEEPS):
        for s in range(subzones):
            old = [[field_ref[t, s, p, k] for k in range(entries)] for p in range(2)]
            sten = [stencil(old[p]) for p in range(2)]
            for k in range(entries):
                alpha, beta, gamma = coef_ref[s, 0, k], coef_ref[s, 1, k], coef_ref[s, 2, k]
                sr, si = sten[0][k], sten[1][k]
                sten_ref[t, s, 0, k] = sr
                sten_ref[t, s, 1, k] = si
                new_real = alpha * old[0][k] - (beta * sr - gamma * si)
                new_imag = alpha * old[1][k] - (beta * si + gamma * sr)
                if t + 1 < SWEEPS:
                    field_ref[t + 1, s, 0, k] = new_real
                    field_ref[t + 1, s, 1, k] = new_imag
                else:
                    lam_ref[s, 0, k] = new_real - field_ref[0, s, 0, k]
                    lam_ref[s, 1, k] = new_imag - field_ref[0, s, 1, k]

    for t in reversed(range(SWEEPS)):
        for s in range(subzones):
            back = [[], []]
            lams = [[lam_ref[s, p, k] for k in range(entries)] for p in range(2)]
            for k in range(entries):
                lr, li = lams[0][k], lams[1][k]
                fr, fi = field_ref[t, s, 0, k], field_ref[t, s, 1, k]
                sr, si = sten_ref[t, s, 0, k], sten_ref[t, s, 1, k]
                g_alpha = lr * fr + li * fi
                g_beta = lr * sr + li * si
                g_gamma = lr * si - li * sr
                if t + 1 < SWEEPS:
                    g_alpha = g_alpha + grad_ref[s, 0, k]
                    g_beta = g_beta + grad_ref[s, 1, k]
                    g_gamma = g_gamma + grad_ref[s, 2, k]
                grad_ref[s, 0, k] = g_alpha
                grad_ref[s, 1, k] = g_beta
                grad_ref[s, 2, k] = g_gamma
                if t > 0:
                    beta, gamma = coef_ref[s, 1, k], coef_ref[s, 2, k]
                    back[0].append(beta * lr + gamma * li)
                    back[1].append(beta * li - gamma * lr)
            if t > 0:
                for p in range(2):
                    sten = stencil(back[p])
                    for k in range(entries):
                        lam_ref[s, p, k] = coef_ref[s, 0, k] * lams[p][k] - sten[k]

    out_ref[...] = jnp.zeros_like(out_ref)
    for s in range(subzones):
        for k in range(entries):
            q = brick_ref[s, k]
            pair = data_ref[q // cap, q % cap]
            shear, damping = pair[0], pair[1]
            diag = 6.0 * shear + wave
            rate = relax_rate / diag
            g_alpha, g_beta, g_gamma = grad_ref[s, 0, k], grad_ref[s, 1, k], grad_ref[s, 2, k]
            mixed = damping * g_gamma - g_beta
            g_rate = wave * g_alpha + shear * mixed
            g_shear = rate * (mixed - 6.0 * g_rate / diag)
            g_damping = rate * shear * g_gamma
            for y in range(out_ref.shape[1]):
                out_ref[q // cap, y, q % cap, 0] += 2.0 * g_shear
                out_ref[q // cap, y, q % cap, 1] += 2.0 * g_damping


def update_kernel(
    freq_count, send_ref, mine_ref, other_ref, data_ref, modulus_ref, first_ref, second_ref, fiber_ref,
    modulus_out, first_out, second_out, total_ref, use_ref,
):
    cap, zones = send_ref.shape
    owned = modulus_ref.shape[0]
    lane = lax.broadcasted_iota(jnp.int32, (SUBL, LANES), 1)
    z_first = lane % BZ == 0
    z_last = lane % BZ == BZ - 1
    total_ref[...] = jnp.zeros_like(total_ref)
    use_ref[...] = jnp.zeros_like(use_ref)
    for d in range(zones):
        for c in range(cap):
            local = send_ref[c, d]
            local = jnp.where(local < 0, owned, local)
            got = total_ref[local]
            for y in range(mine_ref.shape[1]):
                got = got + (mine_ref[d, y, c] + other_ref[d, y, c])
            total_ref[local] = got
            use_ref[local] += data_ref[d, cap + c // 2, c % 2]
    for b in range(owned):
        fib = fiber_ref[b]
        fib_sq = fib * fib
        g_shear, g_damping = total_ref[b, 0], total_ref[b, 1]
        share = 1.0 / (freq_count * jnp.maximum(use_ref[b], 1.0))
        for p, grad in enumerate((g_shear * (1.0 - fib_sq), g_shear * fib_sq, g_damping)):
            descent = grad * share
            new_first = beta_first * first_ref[b, p] + (1.0 - beta_first) * descent
            new_second = beta_second * second_ref[b, p] + (1.0 - beta_second) * descent * descent
            stepped = modulus_ref[b, p] - learn_rate * new_first / (jnp.sqrt(new_second) + adam_eps)
            lower = jnp.where(z_first, stepped, pltpu.roll(stepped, 1, 1))
            upper = jnp.where(z_last, stepped, pltpu.roll(stepped, LANES - 1, 1))
            first_out[b, p] = new_first
            second_out[b, p] = new_second
            modulus_out[b, p] = stepped + smooth_rate * fib_sq * (0.5 * (lower + upper) - stepped)


def on_device(modulus, first_moment, second_moment, fiber, measured, wave_sq, send_list, brick_list):
    zones = lax.axis_size("zone")
    lines = lax.axis_size("line")
    cores = lax.axis_size("core")
    owned = modulus.shape[0]
    cells = (SUBL, LANES)
    cap = send_list.shape[2]
    subzones = brick_list.shape[0]
    send_table = send_list[0].T
    planes = lambda a: a.reshape(owned, 3, *cells)
    mod, first, second = planes(modulus), planes(first_moment), planes(second_moment)
    fib = fiber.reshape(owned, *cells)
    seen = measured.reshape(subzones, 2, K, SUBL, LANES).swapaxes(2, 3).reshape(-1, LANES)
    f32 = jnp.float32
    spare = (cap + 1) // 2
    outgoing = pl.pallas_call(
        pack_kernel,
        out_shape=jax.ShapeDtypeStruct((zones, cap + spare, 2, *cells), f32),
        in_specs=[SMEM, SMEM, VMEM, VMEM],
        out_specs=VMEM,
        scratch_shapes=[pltpu.VMEM((owned, 2, *cells), f32)],
        name="pack",
    )(send_table, brick_list, mod, fib)
    arrived = lax.all_to_all(outgoing, "zone", split_axis=0, concat_axis=0, tiled=True)
    state = (subzones, 2, K, *cells)
    slots = pl.pallas_call(
        solve_kernel,
        out_shape=jax.ShapeDtypeStruct((zones, lines, cap, 2, *cells), f32),
        in_specs=[SMEM, SMEM, VMEM, VMEM],
        out_specs=VMEM,
        scratch_shapes=[
            pltpu.VMEM((subzones, 3, K, *cells), f32),
            pltpu.VMEM((SWEEPS, *state), f32),
            pltpu.VMEM((SWEEPS, *state), f32),
            pltpu.VMEM(state, f32),
            pltpu.VMEM((subzones, 3, K, *cells), f32),
        ],
        name="solve",
    )(brick_list, wave_sq, arrived, seen)
    slots = slots.reshape(zones * lines, cap, 2, *cells)
    mine = lax.all_to_all(slots, ("zone", "line"), split_axis=0, concat_axis=0, tiled=True)
    if cores == 2:
        other = lax.ppermute(mine, "core", [(0, 1), (1, 0)])
    else:
        other = jnp.zeros_like(mine)
    mine, other = (a.reshape(zones, lines, cap, 2, *cells) for a in (mine, other))
    whole = jax.ShapeDtypeStruct((owned, 3, *cells), f32)
    results = pl.pallas_call(
        functools.partial(update_kernel, float(lines * cores)),
        out_shape=(whole, whole, whole),
        in_specs=[SMEM] + [VMEM] * 7,
        out_specs=(VMEM, VMEM, VMEM),
        scratch_shapes=[
            pltpu.VMEM((owned + 1, 2, *cells), f32),
            pltpu.VMEM((owned + 1, *cells), f32),
        ],
        name="update",
    )(send_table, mine, other, arrived, mod, first, second, fib)
    return tuple(r.reshape(modulus.shape) for r in results)


def solution(mesh):
    zones, freqs = mesh.shape["zone"], mesh.shape["freq"]
    cores = 2 if freqs % 2 == 0 else 1
    fine = Mesh(mesh.devices.reshape(zones, freqs // cores, cores), ("zone", "line", "core"))
    freq = ("line", "core")
    brick = P("zone", None, None, None)
    placed = (brick, brick, brick, P("zone", None, None), P(freq, "zone", None, None, None), P(freq), P("zone", None, None), P("zone", None))
    return jax.shard_map(on_device, mesh=fine, in_specs=placed, out_specs=(brick, brick, brick), check_vma=False)
```

time: 277 us -> 41.8 us (0.15)
  local copies, waits for them, and re-layouts: 112 us -> 1.37 us
  other arithmetic: 85.3 us -> 0 us
  waiting for transfers between devices: 25.8 us -> 8.83 us
  between operations: 14.1 us -> 1.29 us
  starting transfers between devices: 16.4 us -> 7.28 us
  Pallas kernels: 0 us -> 8.77 us
    another operation x100 -> x0, local copies, waits for them, and re-layouts: 38.5 us -> none  [misfit(): jnp.stack([resid_real, resid_imag])]
    squeeze x80 -> x0, local copies, waits for them, and re-layouts: 37.3 us -> none  [the longest x24 17.4 us: misfit(): stencil[0] - damping * stencil[1]]
    sub x72 -> x0, other arithmetic: 22.4 us -> none  [the longest x24 14.6 us: misfit(): shear * (stencil[0] - damping * stencil[1]) - wave_value * field[0]]
    another operation x20 -> x0, other arithmetic: 20.5 us -> none  [misfit(): jnp.stack([resid_real, resid_imag])]
    mul x30 -> x0, other arithmetic: 17.6 us -> none  [the longest x24 10.9 us: misfit(): relax_rate * jnp.stack([resid_real, resid_imag]) / diagonal_term]
    all_gather x3 -> x0, blocking collectives: 16 us -> none  [the longest x1 5.33 us: on_device(): lax.all_gather(smoothed, 'freq', axis=3, tiled=True)]
    while x260 -> x0, local copies, waits for them, and re-layouts: 14.2 us -> none
    all_to_all x0 -> x1, blocking collectives: none -> 13.8 us  [on_device(): lax.all_to_all(slots, ('zone', 'line'), split_axis=0, concat_axis=0, tile...]
  transfers between devices with their start and end apart: 4 -> 2, of which waited for: 4 -> 2; matrix products, arithmetic and copies ran while one was open for 1% -> 0% of each run, Pallas kernels for 0% -> 0%
where the time goes in v1:
time: 41.8 us; the launch traced here: 41.4 us
  blocking collectives  13.8 us (33%)
  waiting for transfers between devices  8.83 us (21%)
  Pallas kernels  8.77 us (21%)
  starting transfers between devices  7.28 us (17%)
  local copies, waits for them, and re-layouts  1.37 us (3%)
  between operations  1.29 us (3%)
    all_to_all x1, blocking collectives, on_device(): lax.all_to_all(slots, ('zone', 'line'), split_axis=0, concat_axis=0, tile...  13.8 us
    all_to_all x1, waiting for transfers between devices, on_device(): lax.all_to_all(outgoing, 'zone', split_axis=0, concat_axis=0, tiled=True)  7.3 us
    all_to_all x1, starting transfers between devices, on_device(): lax.all_to_all(outgoing, 'zone', split_axis=0, concat_axis=0, tiled=True)  7.28 us
    pallas_call x1, Pallas kernels, on_device(): pl.pallas_call(solve_kernel, out_shape=jax.ShapeDtypeStruct((zones, lines...  4.94 us
    pallas_call x1, Pallas kernels, on_device(): pl.pallas_call(functools.partial(update_kernel, float(lines * cores)), ou...  2.12 us
    pallas_call x1, Pallas kernels, on_device(): pl.pallas_call(pack_kernel, out_shape=jax.ShapeDtypeStruct((zones, cap +...  1.71 us
    ppermute x1, waiting for transfers between devices, on_device(): other = lax.ppermute(mine, 'core', [(0, 1), (1, 0)])  1.53 us
    unnamed x6, local copies, waits for them, and re-layouts  1.37 us
  transfers between devices with their start and end apart: 2, of which 2 were waited for; matrix products, arithmetic and copies ran while one was open for 0% of the time, Pallas kernels for 0%

profile of v1, /device:TPU:0, one launch (start us, length us, event | category | flops | bytes accessed | tf_op | source)
XLA Modules:
  0.0 41.4 jit_solution(10624038876168882111)
XLA Ops:
  0.6 1.7 %pack.1 = f32[8,3,2,8,128]{4,3,2,1,0:T(8,128)} custom-call(s32[2,8]{1,0:T(2,128)} %bitcast.28, s32[4,8]{1,0:T(4,128)} %brick_ref.3, f32[8,3,8,128]{3,2,1,0:T(8,128)} %bitcast.20, f32[8,8,128]{2,1,0:T(8,128)} %bitcast.24), custom_call_target="tpu_custom_call" | custom-call | tf_op jit(solution)/shard_map/pack/pallas_call | solution.py:216
  2.3 7.3 %all-to-all-start = ((f32[8,3,2,8,128]{4,3,2,1,0:T(8,128)}), f32[8,3,2,8,128]{4,3,2,1,0:T(8,128)S(1)}, u32[]{:S(2)}, u32[]{:S(2)}) async-start(f32[8,3,2,8,128]{4,3,2,1,0:T(8,128)} %pack.1), calls=%async_computation | async-start | bytes 393216 | tf_op jit(solution)/shard_map/all_to_all | solution.py:224
  10.3 7.3 %all-to-all-done.data_ref = f32[8,3,2,8,128]{4,3,2,1,0:T(8,128)S(1)} async-done(((f32[8,3,2,8,128]{4,3,2,1,0:T(8,128)}), f32[8,3,2,8,128]{4,3,2,1,0:T(8,128)S(1)}, u32[]{:S(2)}, u32[]{:S(2)}) %all-to-all-start) | async-done | bytes 196640 | tf_op jit(solution)/shard_map/all_to_all | solution.py:224
  17.6 0.0 copy-start
  17.6 0.7 %copy-done = f32[8,3,2,8,128]{4,3,2,1,0:T(8,128)} copy-done((f32[8,3,2,8,128]{4,3,2,1,0:T(8,128)}, f32[8,3,2,8,128]{4,3,2,1,0:T(8,128)S(1)}, u32[]{:S(2)}) %copy-start) | copy-done | bytes 196632
  18.2 4.9 %solve.1 = f32[8,2,2,2,8,128]{5,4,3,2,1,0:T(8,128)} custom-call(s32[4,8]{1,0:T(4,128)} %brick_ref.3, f32[1]{0:T(128)S(6)} %copy.26.wave_ref, f32[8,3,2,8,128]{4,3,2,1,0:T(8,128)} %copy-done, f32[512,128]{1,0:T(8,128)} %bitcast.23), custom_call_target="tpu_custom_call" | custom-call | tf_op jit(solution)/shard_map/solve/pallas_call | solution.py:226
  23.2 13.8 %all_to_all.10 = f32[16,2,2,8,128]{4,3,2,1,0:T(8,128)S(1)} all-to-all(f32[16,2,2,8,128]{4,3,2,1,0:T(8,128)} %bitcast.19), channel_id=1, replica_groups=mesh['zone'=8,'line'=2,'core'=2] {'zone','line'}, dimensions={0} | all-to-all | bytes 524288 | tf_op jit(solution)/shard_map/all_to_all | solution.py:241
  37.0 0.0 copy-start.1
  37.0 0.0 collective-permute-start
  37.0 1.5 %collective-permute-done = f32[16,2,2,8,128]{4,3,2,1,0:T(8,128)S(1)} collective-permute-done((f32[16,2,2,8,128]{4,3,2,1,0:T(8,128)S(1)}, f32[16,2,2,8,128]{4,3,2,1,0:T(8,128)S(1)}, u32[]{:S(2)}, u32[]{:S(2)}) %collective-permute-start) | collective-permute-done | bytes 262176 | tf_op jit(solution)/shard_map/ppermute | solution.py:243
  38.6 0.0 copy-start.2
  38.6 0.0 copy-done.1
  38.6 0.7 %copy-done.2 = f32[16,2,2,8,128]{4,3,2,1,0:T(8,128)} copy-done((f32[16,2,2,8,128]{4,3,2,1,0:T(8,128)}, f32[16,2,2,8,128]{4,3,2,1,0:T(8,128)S(1)}, u32[]{:S(2)}) %copy-start.2) | copy-done | bytes 262168
  39.3 2.1 %update.1 = (f32[8,3,8,128]{3,2,1,0:T(8,128)}, f32[8,3,8,128]{3,2,1,0:T(8,128)}, f32[8,3,8,128]{3,2,1,0:T(8,128)}) custom-call(s32[2,8]{1,0:T(2,128)} %bitcast.29, f32[8,2,2,2,8,128]{5,4,3,2,1,0:T(8,128)} %bitcast.18, f32[8,2,2,2,8,128]{5,4,3,2,1,0:T(8,128)} %bitcast.22, f32[8,3,2,8,128]{4,3,2,1,0:T(8,128)} %copy-done, f32[8,3,8,128]{3,2,1,0:T(8,128)} %bitcast.21, ...), custom_call_target="tpu_custom_call" | custom-call | tf_op jit(solution)/shard_map/update/pallas_call | solution.py:248
Async XLA Ops:
  2.3 15.2 %all-to-all-start = ((f32[8,3,2,8,128]{4,3,2,1,0:T(8,128)}), f32[8,3,2,8,128]{4,3,2,1,0:T(8,128)S(1)}, u32[]{:S(2)}, u32[]{:S(2)}) async-start(f32[8,3,2,8,128]{4,3,2,1,0:T(8,128)} %pack.1), calls=%async_computation | async-start | bytes 393216 | tf_op jit(solution)/shard_map/all_to_all | solution.py:224
  17.6 0.7 %copy-start = (f32[8,3,2,8,128]{4,3,2,1,0:T(8,128)}, f32[8,3,2,8,128]{4,3,2,1,0:T(8,128)S(1)}, u32[]{:S(2)}) copy-start(f32[8,3,2,8,128]{4,3,2,1,0:T(8,128)S(1)} %all-to-all-done.data_ref) | copy-start | bytes 589828
  37.0 1.5 %copy-start.1 = (f32[16,2,2,8,128]{4,3,2,1,0:T(8,128)}, f32[16,2,2,8,128]{4,3,2,1,0:T(8,128)S(1)}, u32[]{:S(2)}) copy-start(f32[16,2,2,8,128]{4,3,2,1,0:T(8,128)S(1)} %all_to_all.10) | copy-start | bytes 786436
  37.0 1.5 %collective-permute-start = (f32[16,2,2,8,128]{4,3,2,1,0:T(8,128)S(1)}, f32[16,2,2,8,128]{4,3,2,1,0:T(8,128)S(1)}, u32[]{:S(2)}, u32[]{:S(2)}) collective-permute-start(f32[16,2,2,8,128]{4,3,2,1,0:T(8,128)S(1)} %all_to_all.10), channel_id=1, source_target_pairs={{0,1},{1,0},{2,3},{3,2},{4,5},{5,4},{6,7},{7,6},{8,9},{9,8},{10,11... | collective-permute-start | bytes 786440 | tf_op jit(solution)/shard_map/ppermute | solution.py:243
  38.6 0.7 %copy-start.2 = (f32[16,2,2,8,128]{4,3,2,1,0:T(8,128)}, f32[16,2,2,8,128]{4,3,2,1,0:T(8,128)S(1)}, u32[]{:S(2)}) copy-start(f32[16,2,2,8,128]{4,3,2,1,0:T(8,128)S(1)} %collective-permute-done) | copy-start | bytes 786436

commit v2 on v1

--- a/solution.py
+++ b/solution.py
@@ -22,6 +22,10 @@
 
 VMEM = pl.BlockSpec(memory_space=pltpu.VMEM)
 SMEM = pl.BlockSpec(memory_space=pltpu.SMEM)
+
+
+def room(words):
+    return pltpu.CompilerParams(vmem_limit_bytes=4 * words + 2**21)
 
 
 def pack_kernel(send_ref, brick_ref, modulus_ref, fiber_ref, out_ref, plane_ref):
@@ -213,6 +217,8 @@
     seen = measured.reshape(subzones, 2, K, SUBL, LANES).swapaxes(2, 3).reshape(-1, LANES)
     f32 = jnp.float32
     spare = (cap + 1) // 2
+    outgoing_size = zones * (cap + spare) * 2 * SUBL * LANES
+    slot_size = zones * lines * cap * 2 * SUBL * LANES
     outgoing = pl.pallas_call(
         pack_kernel,
         out_shape=jax.ShapeDtypeStruct((zones, cap + spare, 2, *cells), f32),
@@ -235,6 +241,7 @@
             pltpu.VMEM(state, f32),
             pltpu.VMEM((subzones, 3, K, *cells), f32),
         ],
+        compiler_params=room(16 * SWEEPS * seen.size // 4 + 2 * outgoing_size + 2 * slot_size),
         name="solve",
     )(brick_list, wave_sq, arrived, seen)
     slots = slots.reshape(zones * lines, cap, 2, *cells)
@@ -254,6 +261,7 @@
             pltpu.VMEM((owned + 1, 2, *cells), f32),
             pltpu.VMEM((owned + 1, *cells), f32),
         ],
+        compiler_params=room(10 * modulus.size + outgoing_size + 2 * slot_size),
         name="update",
     )(send_table, mine, other, arrived, mod, first, second, fib)
     return tuple(r.reshape(modulus.shape) for r in results)

time: 41.8 us -> 39.3 us (0.940)
  Pallas kernels: 8.77 us -> 6.92 us
  local copies, waits for them, and re-layouts: 1.37 us -> 0.69 us
    pallas_call x1, Pallas kernels: 4.94 us -> 3.75 us  [on_device(): pl.pallas_call(solve_kernel, out_shape=jax.ShapeDtypeStruct((zones, lines...]
    unnamed x6 -> x14, local copies, waits for them, and re-layouts: 1.37 us -> 0.69 us
    pallas_call x1, Pallas kernels: 2.12 us -> 1.46 us  [on_device(): pl.pallas_call(functools.partial(update_kernel, float(lines * cores)), ou...]
where the time goes in v2:
time: 39.3 us; the launch traced here: 39 us
  blocking collectives  13.8 us (35%)
  waiting for transfers between devices  8.82 us (22%)
  starting transfers between devices  7.41 us (19%)
  Pallas kernels  6.92 us (18%)
  between operations  1.35 us (3%)
  local copies, waits for them, and re-layouts  0.69 us (2%)
    all_to_all x1, blocking collectives, on_device(): lax.all_to_all(slots, ('zone', 'line'), split_axis=0, concat_axis=0, tile...  13.8 us
    all_to_all x1, starting transfers between devices, on_device(): lax.all_to_all(outgoing, 'zone', split_axis=0, concat_axis=0, tiled=True)  7.41 us
    all_to_all x1, waiting for transfers between devices, on_device(): lax.all_to_all(outgoing, 'zone', split_axis=0, concat_axis=0, tiled=True)  7.29 us
    pallas_call x1, Pallas kernels, on_device(): pl.pallas_call(solve_kernel, out_shape=jax.ShapeDtypeStruct((zones, lines...  3.75 us
    pallas_call x1, Pallas kernels, on_device(): pl.pallas_call(pack_kernel, out_shape=jax.ShapeDtypeStruct((zones, cap +...  1.71 us
    ppermute x1, waiting for transfers between devices, on_device(): other = lax.ppermute(mine, 'core', [(0, 1), (1, 0)])  1.53 us
    pallas_call x1, Pallas kernels, on_device(): pl.pallas_call(functools.partial(update_kernel, float(lines * cores)), ou...  1.46 us
  transfers between devices with their start and end apart: 2, of which 2 were waited for; matrix products, arithmetic and copies ran while one was open for 0% of the time, Pallas kernels for 0%

profile of v2, /device:TPU:0, one launch (start us, length us, event | category | flops | bytes accessed | tf_op | source)
XLA Modules:
  0.0 39.0 jit_solution(15449219934394790923)
XLA Ops:
  0.6 1.7 %pack.1 = f32[8,3,2,8,128]{4,3,2,1,0:T(8,128)} custom-call(s32[2,8]{1,0:T(2,128)} %bitcast.28, s32[4,8]{1,0:T(4,128)} %brick_ref.3, f32[8,3,8,128]{3,2,1,0:T(8,128)} %bitcast.20, f32[8,8,128]{2,1,0:T(8,128)} %bitcast.24), custom_call_target="tpu_custom_call" | custom-call | tf_op jit(solution)/shard_map/pack/pallas_call | solution.py:222
  2.3 0.0 copy-start.1
  2.3 7.4 %all-to-all-start = ((f32[8,3,2,8,128]{4,3,2,1,0:T(8,128)}), f32[8,3,2,8,128]{4,3,2,1,0:T(8,128)S(1)}, u32[]{:S(2)}, u32[]{:S(2)}) async-start(f32[8,3,2,8,128]{4,3,2,1,0:T(8,128)} %pack.1), calls=%async_computation | async-start | bytes 393216 | tf_op jit(solution)/shard_map/all_to_all | solution.py:230
  9.8 0.0 copy-start.5
  10.4 7.3 %all-to-all-done.data_ref = f32[8,3,2,8,128]{4,3,2,1,0:T(8,128)S(1)} async-done(((f32[8,3,2,8,128]{4,3,2,1,0:T(8,128)}), f32[8,3,2,8,128]{4,3,2,1,0:T(8,128)S(1)}, u32[]{:S(2)}, u32[]{:S(2)}) %all-to-all-start) | async-done | bytes 196640 | tf_op jit(solution)/shard_map/all_to_all | solution.py:230
  17.7 0.0 copy-done.1
  17.7 0.0 copy-done.5
  17.7 3.7 %solve.1 = f32[8,2,2,2,8,128]{5,4,3,2,1,0:T(8,128)S(1)} custom-call(s32[4,8]{1,0:T(4,128)S(1)} %copy-done.5, f32[1]{0:T(128)S(6)} %copy.26.wave_ref, f32[8,3,2,8,128]{4,3,2,1,0:T(8,128)S(1)} %all-to-all-done.data_ref, f32[512,128]{1,0:T(8,128)S(1)} %bitcast.23), custom_call_target="tpu_custom_call" | custom-call | tf_op jit(solution)/shard_map/solve/pallas_call | solution.py:232
  21.5 0.0 copy-start
  21.5 0.0 copy-start.2
  21.5 0.0 copy-start.3
  21.5 0.0 copy-start.4
  21.5 13.8 %all_to_all.10 = f32[16,2,2,8,128]{4,3,2,1,0:T(8,128)S(1)} all-to-all(f32[16,2,2,8,128]{4,3,2,1,0:T(8,128)S(1)} %bitcast.19), channel_id=1, replica_groups=mesh['zone'=8,'line'=2,'core'=2] {'zone','line'}, dimensions={0} | all-to-all | bytes 524288 | tf_op jit(solution)/shard_map/all_to_all | solution.py:248
  35.3 0.0 collective-permute-start
  35.3 1.5 %collective-permute-done = f32[16,2,2,8,128]{4,3,2,1,0:T(8,128)S(1)} collective-permute-done((f32[16,2,2,8,128]{4,3,2,1,0:T(8,128)S(1)}, f32[16,2,2,8,128]{4,3,2,1,0:T(8,128)S(1)}, u32[]{:S(2)}, u32[]{:S(2)}) %collective-permute-start) | collective-permute-done | bytes 262176 | tf_op jit(solution)/shard_map/ppermute | solution.py:250
  36.8 0.0 copy-start.6
  36.8 0.0 copy-done
  36.8 0.0 copy-done.2
  36.8 0.0 copy-done.3
  36.8 0.0 copy-done.4
  36.8 0.7 %copy-done.6 = s32[1,8,2]{1,2,0:T(2,128)S(1)} copy-done((s32[1,8,2]{1,2,0:T(2,128)S(1)}, s32[1,8,2]{1,2,0:T(2,128)}, u32[]{:S(2)}) %copy-start.6) | copy-done | bytes 88
  37.5 1.5 %update.1 = (f32[8,3,8,128]{3,2,1,0:T(8,128)}, f32[8,3,8,128]{3,2,1,0:T(8,128)}, f32[8,3,8,128]{3,2,1,0:T(8,128)}) custom-call(s32[2,8]{1,0:T(2,128)S(1)} %bitcast.29, f32[8,2,2,2,8,128]{5,4,3,2,1,0:T(8,128)S(1)} %bitcast.18, f32[8,2,2,2,8,128]{5,4,3,2,1,0:T(8,128)S(1)} %bitcast.22, f32[8,3,2,8,128]{4,3,2,1,0:T(8,128)S(1)} %all-to-all-done.data_ref, ...), custom_call_target="tpu_custom_call" | custom-call | tf_op jit(solution)/shard_map/update/pallas_call | solution.py:255
Async XLA Ops:
  2.3 15.4 %copy-start.1 = (f32[1,4,2,8,1024]{4,3,2,1,0:T(8,128)S(1)}, f32[1,4,2,8,1024]{4,3,2,1,0:T(8,128)}, u32[]{:S(2)}) copy-start(f32[1,4,2,8,1024]{4,3,2,1,0:T(8,128)} %param.12) | copy-start | bytes 786436
  2.3 15.4 %all-to-all-start = ((f32[8,3,2,8,128]{4,3,2,1,0:T(8,128)}), f32[8,3,2,8,128]{4,3,2,1,0:T(8,128)S(1)}, u32[]{:S(2)}, u32[]{:S(2)}) async-start(f32[8,3,2,8,128]{4,3,2,1,0:T(8,128)} %pack.1), calls=%async_computation | async-start | bytes 393216 | tf_op jit(solution)/shard_map/all_to_all | solution.py:230
  9.8 8.0 %copy-start.5 = (s32[4,8]{1,0:T(4,128)S(1)}, s32[4,8]{1,0:T(4,128)}, u32[]{:S(2)}) copy-start(s32[4,8]{1,0:T(4,128)} %brick_ref.3) | copy-start | bytes 388
  21.5 15.4 %copy-start = (f32[8,3,1,1024]{3,2,1,0:T(1,128)S(1)}, f32[8,3,1,1024]{3,2,1,0:T(1,128)}, u32[]{:S(2)}) copy-start(f32[8,3,1,1024]{3,2,1,0:T(1,128)} %param.8) | copy-start | bytes 294916
  21.5 15.3 %copy-start.2 = (f32[8,1,1024]{2,1,0:T(1,128)S(1)}, f32[8,1,1024]{2,1,0:T(1,128)}, u32[]{:S(2)}) copy-start(f32[8,1,1024]{2,1,0:T(1,128)} %param.11) | copy-start | bytes 98308
  21.5 15.3 %copy-start.3 = (f32[8,3,1,1024]{3,2,1,0:T(1,128)S(1)}, f32[8,3,1,1024]{3,2,1,0:T(1,128)}, u32[]{:S(2)}) copy-start(f32[8,3,1,1024]{3,2,1,0:T(1,128)} %param.9) | copy-start | bytes 294916
  21.5 15.3 %copy-start.4 = (f32[8,3,1,1024]{3,2,1,0:T(1,128)S(1)}, f32[8,3,1,1024]{3,2,1,0:T(1,128)}, u32[]{:S(2)}) copy-start(f32[8,3,1,1024]{3,2,1,0:T(1,128)} %param.10) | copy-start | bytes 294916
  35.3 1.5 %collective-permute-start = (f32[16,2,2,8,128]{4,3,2,1,0:T(8,128)S(1)}, f32[16,2,2,8,128]{4,3,2,1,0:T(8,128)S(1)}, u32[]{:S(2)}, u32[]{:S(2)}) collective-permute-start(f32[16,2,2,8,128]{4,3,2,1,0:T(8,128)S(1)} %all_to_all.10), channel_id=1, source_target_pairs={{0,1},{1,0},{2,3},{3,2},{4,5},{5,4},{6,7},{7,6},{8,9},{9,8},{10,11... | collective-permute-start | bytes 786440 | tf_op jit(solution)/shard_map/ppermute | solution.py:250
  36.8 0.7 %copy-start.6 = (s32[1,8,2]{1,2,0:T(2,128)S(1)}, s32[1,8,2]{1,2,0:T(2,128)}, u32[]{:S(2)}) copy-start(s32[1,8,2]{1,2,0:T(2,128)} %param.14) | copy-start | bytes 196

commit v3 on v2

v3 whole, which is shorter than its diff:
```python
import functools

import jax
import jax.numpy as jnp
from jax import lax
from jax.experimental import pallas as pl
from jax.experimental.pallas import tpu as pltpu
from jax.sharding import Mesh, PartitionSpec as P

BZ = 32
K = 8
SWEEPS = 6
LANES = 128
SUBL = 8

relax_rate = 0.25
learn_rate = 0.1
beta_first = 0.9
beta_second = 0.99
smooth_rate = 0.5
adam_eps = 1e-08

VMEM = pl.BlockSpec(memory_space=pltpu.VMEM)
SMEM = pl.BlockSpec(memory_space=pltpu.SMEM)
HBM = pl.BlockSpec(memory_space=pltpu.HBM)


def room(words):
    return pltpu.CompilerParams(vmem_limit_bytes=4 * words + 2**21)


def pack_kernel(
    send_hbm, brick_hbm, modulus_hbm, fiber_hbm,
    out_ref, send_out, brick_out,
    send_ref, brick_ref, modulus_ref, fiber_ref, plane_ref, sems,
):
    pairs = (
        (send_hbm, send_ref), (brick_hbm, brick_ref), (modulus_hbm, modulus_ref), (fiber_hbm, fiber_ref),
        (send_hbm, send_out), (brick_hbm, brick_out),
    )
    copies = [pltpu.make_async_copy(a, b, sems.at[i]) for i, (a, b) in enumerate(pairs)]
    for copy in copies:
        copy.start()
    for copy in copies[:4]:
        copy.wait()
    cap, zones = send_ref.shape
    owned = modulus_ref.shape[0]
    for b in range(owned):
        fib = fiber_ref[b]
        base = modulus_ref[b, 0]
        plane_ref[b, 0] = base + (modulus_ref[b, 1] - base) * fib * fib
        plane_ref[b, 1] = modulus_ref[b, 2]
    slot_at = lax.broadcasted_iota(jnp.int32, (SUBL, LANES), 1)
    for first in range(0, zones * cap, LANES):
        uses = jnp.zeros((SUBL, LANES), jnp.float32)
        for s in range(brick_ref.shape[0]):
            for k in range(brick_ref.shape[1]):
                uses = uses + jnp.where(slot_at == brick_ref[s, k] - first, 1.0, 0.0)
        for q in range(first, min(first + LANES, zones * cap)):
            wide = jnp.broadcast_to(uses[:1, q - first : q - first + 1], (1, LANES))
            row = 2 * SUBL * cap + q % cap
            out_ref[q // cap, row : row + 1] = wide
    for d in range(zones):
        for c in range(cap):
            local = jnp.maximum(send_ref[c, d], 0)
            for p in range(2):
                row = (2 * c + p) * SUBL
                out_ref[d, row : row + SUBL] = plane_ref[local, p]
        row = 2 * SUBL * cap + cap
        if row < out_ref.shape[1]:
            out_ref[d, row:] = jnp.zeros((out_ref.shape[1] - row, LANES), jnp.float32)
    for copy in copies[4:]:
        copy.wait()


def stencil(v, table_ref, res_ref):
    rows = v[0][0].shape[0]
    flat = jnp.concatenate([tile for line in v for tile in line], axis=0)
    high = flat.astype(jnp.bfloat16)
    low = (flat - high.astype(jnp.float32)).astype(jnp.bfloat16)
    res_ref[...] = jnp.dot(
        jnp.concatenate([high, low], axis=1), table_ref[...], preferred_element_type=jnp.float32
    )
    lane = lax.broadcasted_iota(jnp.int32, (rows, LANES), 1)
    low_half = lane < LANES // 2
    res = []
    for x, line in enumerate(v):
        res.append([])
        for y in range(len(line)):
            at = (x * len(line) + y) * rows
            below = res_ref[at - rows : at, LANES:] if y > 0 else 0.0
            above = res_ref[at + rows : at + 2 * rows, LANES:] if y + 1 < len(line) else 0.0
            total = res_ref[at : at + rows, :LANES] + jnp.where(low_half, below, above)
            sides = [v[i][y] for i in (x - 1, x + 1) if 0 <= i < len(v)]
            res[-1].append(total - sum(sides[1:], sides[0]))
    return res


def prepare_kernel(seen_ref, field_out, sten_out, table_out, res_ref):
    source = lax.broadcasted_iota(jnp.int32, table_out.shape, 0) % LANES
    column = lax.broadcasted_iota(jnp.int32, table_out.shape, 1)
    target = column % LANES
    step = jnp.abs(source - target)
    beside = jnp.logical_or(step == BZ, jnp.logical_and(step == 1, source // BZ == target // BZ))
    inner = jnp.where(step == 0, 6.0, jnp.where(beside, -1.0, 0.0))
    wrap = jnp.where(step == LANES - BZ, -1.0, 0.0)
    table_out[...] = jnp.where(column < LANES, inner, wrap).astype(table_out.dtype)
    lines, subl, rows, _ = field_out.shape
    subzones = rows // 2
    for x in range(lines):
        for y in range(subl):
            for p in range(2):
                at = p * subl * lines + y * lines + x
                field_out[x, y, p * subzones : (p + 1) * subzones] = seen_ref[
                    pl.ds(at, subzones, stride=2 * subl * lines), :
                ]
    sten = stencil([[field_out[x, y] for y in range(subl)] for x in range(lines)], table_out, res_ref)
    for x in range(lines):
        for y in range(subl):
            sten_out[x, y] = sten[x][y]


def solve_kernel(
    brick_ref, wave_ref, data_ref, start_ref, sten0_ref, table_ref, out_ref,
    coef_ref, field_ref, sten_ref, lam_ref, grad_ref, res_ref, sum_ref,
):
    subzones, entries = brick_ref.shape
    rows = 2 * subzones
    cap = out_ref.shape[2]
    slots = out_ref.shape[0] * cap
    wave = wave_ref[0]
    grid = [(x, y) for x in range(entries) for y in range(SUBL)]

    def swap(v):
        return pltpu.roll(v, subzones, 0)

    def moduli(s, k):
        q = brick_ref[s, k]
        shear = data_ref[q // cap, pl.ds(pl.multiple_of(q % cap * 2 * SUBL, SUBL), SUBL)]
        damping = data_ref[q // cap, pl.ds(pl.multiple_of((q % cap * 2 + 1) * SUBL, SUBL), SUBL)]
        return shear, damping

    def rows_of(p, s, k):
        return pl.ds(k * SUBL * rows + p * subzones + s, SUBL, stride=rows)

    for s in range(subzones):
        for k in range(entries):
            shear, damping = moduli(s, k)
            rate = relax_rate / (6.0 * shear + wave)
            alpha = 1.0 + rate * wave
            beta = rate * shear
            gamma = beta * damping
            for p in range(2):
                coef_ref[0, rows_of(p, s, k), :] = alpha
                coef_ref[1, rows_of(p, s, k), :] = beta
                coef_ref[2, rows_of(p, s, k), :] = gamma if p == 0 else -gamma

    def coef(i, x, y):
        at = (x * SUBL + y) * rows
        return coef_ref[i, at : at + rows]

    def field(t, x, y):
        return field_ref[t - 1, x, y] if t > 0 else start_ref[x, y]

    for t in range(SWEEPS):
        if t == 0:
            sten = [[sten0_ref[x, y] for y in range(SUBL)] for x in range(entries)]
        else:
            sten = stencil([[field(t, x, y) for y in range(SUBL)] for x in range(entries)], table_ref, res_ref)
        for x, y in grid:
            own = sten[x][y]
            turned = swap(own)
            sten_ref[t, 0, x, y] = own
            sten_ref[t, 1, x, y] = turned
            new = coef(0, x, y) * field(t, x, y) - coef(1, x, y) * own + coef(2, x, y) * turned
            if t + 1 < SWEEPS:
                field_ref[t, x, y] = new
            else:
                lam_ref[x, y] = new - start_ref[x, y]

    for t in reversed(range(SWEEPS)):
        back = [[None] * SUBL for _ in range(entries)]
        for x, y in grid:
            lam = lam_ref[x, y]
            parts = (lam * field(t, x, y), lam * sten_ref[t, 0, x, y], lam * sten_ref[t, 1, x, y])
            at = (x * SUBL + y) * rows
            for i, part in enumerate(parts):
                if t + 1 < SWEEPS:
                    part = part + grad_ref[i, at : at + rows]
                grad_ref[i, at : at + rows] = part
            if t > 0:
                back[x][y] = coef(1, x, y) * lam + coef(2, x, y) * swap(lam)
        if t > 0:
            sten = stencil(back, table_ref, res_ref)
            for x, y in grid:
                lam_ref[x, y] = coef(0, x, y) * lam_ref[x, y] - sten[x][y]

    sum_ref[...] = jnp.zeros_like(sum_ref)
    for s in range(subzones):
        for k in range(entries):
            shear, damping = moduli(s, k)
            diag = 6.0 * shear + wave
            rate = relax_rate / diag
            real, imag = ([grad_ref[i, rows_of(p, s, k), :] for i in range(3)] for p in range(2))
            g_alpha, g_beta, g_gamma = real[0] + imag[0], real[1] + imag[1], real[2] - imag[2]
            mixed = damping * g_gamma - g_beta
            g_rate = wave * g_alpha + shear * mixed
            q = brick_ref[s, k]
            sum_ref[s, q, 0] += rate * (mixed - 6.0 * g_rate / diag)
            sum_ref[s, q, 1] += rate * shear * g_gamma
    for q in range(slots):
        for p in range(2):
            total = sum_ref[0, q, p]
            for s in range(1, subzones):
                total = total + sum_ref[s, q, p]
            total = 2.0 * total
            for y in range(out_ref.shape[1]):
                out_ref[q // cap, y, q % cap, p] = total


def update_kernel(
    freq_count, send_ref, mine_ref, other_ref, data_ref, modulus_ref, first_ref, second_ref, fiber_ref,
    modulus_out, first_out, second_out, total_ref, use_ref,
):
    cap, zones = send_ref.shape
    owned = modulus_ref.shape[0]
    lane = lax.broadcasted_iota(jnp.int32, (SUBL, LANES), 1)
    z_first = lane % BZ == 0
    z_last = lane % BZ == BZ - 1
    total_ref[...] = jnp.zeros_like(total_ref)
    use_ref[...] = jnp.zeros_like(use_ref)
    for d in range(zones):
        for c in range(cap):
            local = send_ref[c, d]
            local = jnp.where(local < 0, owned, local)
            got = total_ref[local]
            for y in range(mine_ref.shape[1]):
                got = got + (mine_ref[d, y, c] + other_ref[d, y, c])
            total_ref[local] = got
            use_ref[local] += data_ref[d, pl.ds(2 * SUBL * cap + c, 1)]
    for b in range(owned):
        fib = fiber_ref[b]
        fib_sq = fib * fib
        g_shear, g_damping = total_ref[b, 0], total_ref[b, 1]
        share = 1.0 / (freq_count * jnp.maximum(use_ref[b], 1.0))
        for p, grad in enumerate((g_shear * (1.0 - fib_sq), g_shear * fib_sq, g_damping)):
            descent = grad * share
            new_first = beta_first * first_ref[b, p] + (1.0 - beta_first) * descent
            new_second = beta_second * second_ref[b, p] + (1.0 - beta_second) * descent * descent
            stepped = modulus_ref[b, p] - learn_rate * new_first / (jnp.sqrt(new_second) + adam_eps)
            lower = jnp.where(z_first, stepped, pltpu.roll(stepped, 1, 1))
            upper = jnp.where(z_last, stepped, pltpu.roll(stepped, LANES - 1, 1))
            first_out[b, p] = new_first
            second_out[b, p] = new_second
            modulus_out[b, p] = stepped + smooth_rate * fib_sq * (0.5 * (lower + upper) - stepped)


def on_device(modulus, first_moment, second_moment, fiber, measured, wave_sq, send_list, brick_list):
    zones = lax.axis_size("zone")
    lines = lax.axis_size("line")
    cores = lax.axis_size("core")
    owned = modulus.shape[0]
    cells = (SUBL, LANES)
    cap = send_list.shape[2]
    subzones = brick_list.shape[0]
    planes = lambda a: a.reshape(owned, 3, *cells)
    mod, first, second = planes(modulus), planes(first_moment), planes(second_moment)
    fib = fiber.reshape(owned, *cells)
    seen = measured.reshape(subzones, 2, K, SUBL, LANES).swapaxes(2, 3).reshape(-1, LANES)
    f32 = jnp.float32
    rows = 2 * SUBL * cap + -(-cap // SUBL) * SUBL
    outgoing_size = zones * rows * LANES
    slot_size = zones * lines * cap * 2 * SUBL * LANES
    i32 = jnp.int32
    shape = jax.ShapeDtypeStruct
    outgoing, send_table, bricks = pl.pallas_call(
        pack_kernel,
        out_shape=(
            shape((zones, rows, LANES), f32), shape((cap, zones), i32), shape(brick_list.shape, i32),
        ),
        in_specs=[HBM] * 4,
        out_specs=(VMEM,) * 3,
        scratch_shapes=[
            pltpu.SMEM((cap, zones), i32),
            pltpu.SMEM(brick_list.shape, i32),
            pltpu.VMEM((owned, 3, *cells), f32),
            pltpu.VMEM((owned, *cells), f32),
            pltpu.VMEM((owned, 2, *cells), f32),
            pltpu.SemaphoreType.DMA((6,)),
        ],
        compiler_params=room(outgoing_size + 4 * modulus.size),
        name="pack",
    )(*(pltpu.with_memory_space_constraint(a, pltpu.HBM) for a in (send_list[0].T, brick_list, mod, fib)))
    arrived = lax.all_to_all(outgoing, "zone", split_axis=0, concat_axis=0, tiled=True)
    state = (K, SUBL, 2 * subzones, LANES)
    sites = K * SUBL * 2 * subzones
    table = (2 * LANES, 2 * LANES)
    start, sten0, neighbours = pl.pallas_call(
        prepare_kernel,
        out_shape=(shape(state, f32), shape(state, f32), shape(table, jnp.bfloat16)),
        in_specs=[VMEM],
        out_specs=(VMEM,) * 3,
        scratch_shapes=[pltpu.VMEM((sites, 2 * LANES), f32)],
        compiler_params=room(8 * seen.size),
        cost_estimate=pl.CostEstimate(flops=2**24, bytes_accessed=16 * seen.size, transcendentals=0),
        name="prepare",
    )(seen)
    slots = pl.pallas_call(
        solve_kernel,
        out_shape=shape((zones, lines, cap, 2, *cells), f32),
        in_specs=[SMEM, SMEM] + [VMEM] * 4,
        out_specs=VMEM,
        scratch_shapes=[
            pltpu.VMEM((3, sites, LANES), f32),
            pltpu.VMEM((SWEEPS - 1, *state), f32),
            pltpu.VMEM((SWEEPS, 2, *state), f32),
            pltpu.VMEM(state, f32),
            pltpu.VMEM((3, sites, LANES), f32),
            pltpu.VMEM((sites, 2 * LANES), f32),
            pltpu.VMEM((subzones, zones * cap, 2, *cells), f32),
        ],
        compiler_params=room((8 * SWEEPS + 8) * seen.size + 2 * outgoing_size + (2 + subzones) * slot_size),
        name="solve",
    )(bricks, wave_sq, arrived, start, sten0, neighbours)
    slots = slots.reshape(zones * lines, cap, 2, *cells)
    mine = lax.all_to_all(slots, ("zone", "line"), split_axis=0, concat_axis=0, tiled=True)
    if cores == 2:
        other = lax.ppermute(mine, "core", [(0, 1), (1, 0)])
    else:
        other = jnp.zeros_like(mine)
    mine, other = (a.reshape(zones, lines, cap, 2, *cells) for a in (mine, other))
    whole = jax.ShapeDtypeStruct((owned, 3, *cells), f32)
    results = pl.pallas_call(
        functools.partial(update_kernel, float(lines * cores)),
        out_shape=(whole, whole, whole),
        in_specs=[SMEM] + [VMEM] * 7,
        out_specs=(VMEM, VMEM, VMEM),
        scratch_shapes=[
            pltpu.VMEM((owned + 1, 2, *cells), f32),
            pltpu.VMEM((owned + 1, 1, LANES), f32),
        ],
        compiler_params=room(10 * modulus.size + outgoing_size + 2 * slot_size),
        name="update",
    )(send_table, mine, other, arrived, mod, first, second, fib)
    return tuple(r.reshape(modulus.shape) for r in results)


def solution(mesh):
    zones, freqs = mesh.shape["zone"], mesh.shape["freq"]
    cores = 2 if freqs % 2 == 0 else 1
    fine = Mesh(mesh.devices.reshape(zones, freqs // cores, cores), ("zone", "line", "core"))
    freq = ("line", "core")
    brick = P("zone", None, None, None)
    placed = (brick, brick, brick, P("zone", None, None), P(freq, "zone", None, None, None), P(freq), P("zone", None, None), P("zone", None))
    return jax.shard_map(on_device, mesh=fine, in_specs=placed, out_specs=(brick, brick, brick), check_vma=False)
```

time: 39.3 us -> 36.9 us (0.939)
  waiting for transfers between devices: 8.82 us -> 8 us
  local copies, waits for them, and re-layouts: 0.69 us -> 0.03 us
  Pallas kernels: 6.92 us -> 6.43 us
  blocking collectives: 13.8 us -> 13.4 us
    all_to_all x1, waiting for transfers between devices: 7.29 us -> 6.47 us  [on_device(): lax.all_to_all(outgoing, 'zone', split_axis=0, concat_axis=0, tiled=True)]
    unnamed x14 -> x10, local copies, waits for them, and re-layouts: 0.69 us -> 0.03 us
    pallas_call x2 -> x3, Pallas kernels: 5.46 us -> 4.98 us  [the longest x1 2.75 us: on_device(): pl.pallas_call(solve_kernel, out_shape=shape((zones, lines, cap, 2, *cell...]
  transfers between devices with their start and end apart: 2 -> 2, of which waited for: 2 -> 2; matrix products, arithmetic and copies ran while one was open for 0% -> 0% of each run, Pallas kernels for 0% -> 1%
where the time goes in v3:
time: 36.9 us; the launch traced here: 36.6 us
  blocking collectives  13.4 us (36%)
  waiting for transfers between devices  8 us (22%)
  starting transfers between devices  7.3 us (20%)
  Pallas kernels  6.43 us (17%)
  between operations  1.37 us (4%)
    all_to_all x1, blocking collectives, on_device(): lax.all_to_all(slots, ('zone', 'line'), split_axis=0, concat_axis=0, tile...  13.4 us
    all_to_all x1, starting transfers between devices, on_device(): lax.all_to_all(outgoing, 'zone', split_axis=0, concat_axis=0, tiled=True)  7.29 us
    all_to_all x1, waiting for transfers between devices, on_device(): lax.all_to_all(outgoing, 'zone', split_axis=0, concat_axis=0, tiled=True)  6.47 us
    pallas_call x1, Pallas kernels, on_device(): pl.pallas_call(solve_kernel, out_shape=shape((zones, lines, cap, 2, *cell...  2.75 us
    pallas_call x1, Pallas kernels, on_device(): pl.pallas_call(pack_kernel, out_shape=(shape((zones, rows, LANES), f32),...  1.8 us
    ppermute x1, waiting for transfers between devices, on_device(): other = lax.ppermute(mine, 'core', [(0, 1), (1, 0)])  1.53 us
    pallas_call x1, Pallas kernels, on_device(): pl.pallas_call(functools.partial(update_kernel, float(lines * cores)), ou...  1.45 us
  transfers between devices with their start and end apart: 2, of which 2 were waited for; matrix products, arithmetic and copies ran while one was open for 0% of the time, Pallas kernels for 1%

profile of v3, /device:TPU:0, one launch (start us, length us, event | category | flops | bytes accessed | tf_op | source)
XLA Modules:
  0.0 36.6 jit_solution(1510520522288773282)
XLA Ops:
  0.6 0.0 copy-start.1
  0.6 1.8 %pack.1 = (f32[8,40,128]{2,1,0:T(8,128)}, s32[2,8]{1,0:T(2,128)S(1)}, s32[4,8]{1,0:T(4,128)S(1)}) custom-call(s32[2,8]{1,0:T(2,128)} %bitcast.28, s32[4,8]{1,0:T(4,128)} %brick_hbm.1, f32[8,3,8,128]{3,2,1,0:T(8,128)} %bitcast.20, f32[8,8,128]{2,1,0:T(8,128)} %bitcast.24), custom_call_target="tpu_custom_call" | custom-call | tf_op jit(solution)/shard_map/pack/pallas_call | solution.py:276
  2.4 7.3 %all-to-all-start = ((f32[8,40,128]{2,1,0:T(8,128)}), f32[8,40,128]{2,1,0:T(8,128)S(1)}, u32[]{:S(2)}, u32[]{:S(2)}) async-start(f32[8,40,128]{2,1,0:T(8,128)} %get-tuple-element.14), calls=%async_computation | async-start | bytes 327680 | tf_op jit(solution)/shard_map/all_to_all | solution.py:294
  10.4 0.0 copy-done.1
  10.4 0.4 %prepare.1 = (f32[8,8,8,128]{3,2,1,0:T(8,128)S(1)}, f32[8,8,8,128]{3,2,1,0:T(8,128)S(1)}, bf16[256,256]{1,0:T(8,128)(2,1)S(1)}) custom-call(f32[512,128]{1,0:T(8,128)S(1)} %bitcast.23), custom_call_target="tpu_custom_call" | custom-call | flops 16777216 | bytes 1048576 | tf_op jit(solution)/shard_map/prepare/pallas_call | solution.py:298
  10.8 6.5 %all-to-all-done.data_ref = f32[8,40,128]{2,1,0:T(8,128)S(1)} async-done(((f32[8,40,128]{2,1,0:T(8,128)}), f32[8,40,128]{2,1,0:T(8,128)S(1)}, u32[]{:S(2)}, u32[]{:S(2)}) %all-to-all-start) | async-done | bytes 163872 | tf_op jit(solution)/shard_map/all_to_all | solution.py:294
  17.3 2.8 %solve.1 = f32[8,2,2,2,8,128]{5,4,3,2,1,0:T(8,128)S(1)} custom-call(s32[4,8]{1,0:T(4,128)S(1)} %get-tuple-element.13.brick_ref, f32[1]{0:T(128)S(6)} %copy.26.wave_ref, f32[8,40,128]{2,1,0:T(8,128)S(1)} %all-to-all-done.data_ref, f32[8,8,8,128]{3,2,1,0:T(8,128)S(1)} %get-tuple-element.15.start_ref, f32[8,8,8,128]{3,2,1,0:T(8,128)S(1)} %get-tuple-element.16.sten0_ref, ...), custom_call_target="tpu_custom_call" | custom-call | tf_op jit(solution)/shard_map/solve/pallas_call | solution.py:308
  20.1 0.0 copy-start
  20.1 0.0 copy-start.2
  20.1 0.0 copy-start.3
  20.1 0.0 copy-start.4
  20.1 13.4 %all_to_all.10 = f32[16,2,2,8,128]{4,3,2,1,0:T(8,128)S(1)} all-to-all(f32[16,2,2,8,128]{4,3,2,1,0:T(8,128)S(1)} %bitcast.19), channel_id=1, replica_groups=mesh['zone'=8,'line'=2,'core'=2] {'zone','line'}, dimensions={0} | all-to-all | bytes 524288 | tf_op jit(solution)/shard_map/all_to_all | solution.py:326
  33.6 0.0 collective-permute-start
  33.6 1.5 %collective-permute-done = f32[16,2,2,8,128]{4,3,2,1,0:T(8,128)S(1)} collective-permute-done((f32[16,2,2,8,128]{4,3,2,1,0:T(8,128)S(1)}, f32[16,2,2,8,128]{4,3,2,1,0:T(8,128)S(1)}, u32[]{:S(2)}, u32[]{:S(2)}) %collective-permute-start) | collective-permute-done | bytes 262176 | tf_op jit(solution)/shard_map/ppermute | solution.py:328
  35.1 0.0 copy-done
  35.1 0.0 copy-done.2
  35.1 0.0 copy-done.3
  35.1 0.0 copy-done.4
  35.1 1.4 %update.1 = (f32[8,3,8,128]{3,2,1,0:T(8,128)}, f32[8,3,8,128]{3,2,1,0:T(8,128)}, f32[8,3,8,128]{3,2,1,0:T(8,128)}) custom-call(s32[2,8]{1,0:T(2,128)S(1)} %get-tuple-element.12.send_ref, f32[8,2,2,2,8,128]{5,4,3,2,1,0:T(8,128)S(1)} %bitcast.18, f32[8,2,2,2,8,128]{5,4,3,2,1,0:T(8,128)S(1)} %bitcast.22, f32[8,40,128]{2,1,0:T(8,128)S(1)} %all-to-all-done.data_ref, ...), custom_call_target="tpu_custom_call" | custom-call | tf_op jit(solution)/shard_map/update/pallas_call | solution.py:333
Async XLA Ops:
  0.6 9.8 %copy-start.1 = (f32[1,4,2,8,1024]{4,3,2,1,0:T(8,128)S(1)}, f32[1,4,2,8,1024]{4,3,2,1,0:T(8,128)}, u32[]{:S(2)}) copy-start(f32[1,4,2,8,1024]{4,3,2,1,0:T(8,128)} %param.12) | copy-start | bytes 786436
  2.4 14.9 %all-to-all-start = ((f32[8,40,128]{2,1,0:T(8,128)}), f32[8,40,128]{2,1,0:T(8,128)S(1)}, u32[]{:S(2)}, u32[]{:S(2)}) async-start(f32[8,40,128]{2,1,0:T(8,128)} %get-tuple-element.14), calls=%async_computation | async-start | bytes 327680 | tf_op jit(solution)/shard_map/all_to_all | solution.py:294
  20.1 15.0 %copy-start = (f32[8,3,1,1024]{3,2,1,0:T(1,128)S(1)}, f32[8,3,1,1024]{3,2,1,0:T(1,128)}, u32[]{:S(2)}) copy-start(f32[8,3,1,1024]{3,2,1,0:T(1,128)} %param.8) | copy-start | bytes 294916
  20.1 15.0 %copy-start.2 = (f32[8,1,1024]{2,1,0:T(1,128)S(1)}, f32[8,1,1024]{2,1,0:T(1,128)}, u32[]{:S(2)}) copy-start(f32[8,1,1024]{2,1,0:T(1,128)} %param.11) | copy-start | bytes 98308
  20.1 15.0 %copy-start.3 = (f32[8,3,1,1024]{3,2,1,0:T(1,128)S(1)}, f32[8,3,1,1024]{3,2,1,0:T(1,128)}, u32[]{:S(2)}) copy-start(f32[8,3,1,1024]{3,2,1,0:T(1,128)} %param.9) | copy-start | bytes 294916
  20.1 15.0 %copy-start.4 = (f32[8,3,1,1024]{3,2,1,0:T(1,128)S(1)}, f32[8,3,1,1024]{3,2,1,0:T(1,128)}, u32[]{:S(2)}) copy-start(f32[8,3,1,1024]{3,2,1,0:T(1,128)} %param.10) | copy-start | bytes 294916
  33.6 1.5 %collective-permute-start = (f32[16,2,2,8,128]{4,3,2,1,0:T(8,128)S(1)}, f32[16,2,2,8,128]{4,3,2,1,0:T(8,128)S(1)}, u32[]{:S(2)}, u32[]{:S(2)}) collective-permute-start(f32[16,2,2,8,128]{4,3,2,1,0:T(8,128)S(1)} %all_to_all.10), channel_id=1, source_target_pairs={{0,1},{1,0},{2,3},{3,2},{4,5},{5,4},{6,7},{7,6},{8,9},{9,8},{10,11... | collective-permute-start | bytes 786440 | tf_op jit(solution)/shard_map/ppermute | solution.py:328

commit v4 on v3

--- a/solution.py
+++ b/solution.py
@@ -32,11 +32,11 @@
 def pack_kernel(
     send_hbm, brick_hbm, modulus_hbm, fiber_hbm,
     out_ref, send_out, brick_out,
-    send_ref, brick_ref, modulus_ref, fiber_ref, plane_ref, sems,
+    send_ref, brick_ref, slot_ref, modulus_ref, fiber_ref, plane_ref, sems,
 ):
     pairs = (
         (send_hbm, send_ref), (brick_hbm, brick_ref), (modulus_hbm, modulus_ref), (fiber_hbm, fiber_ref),
-        (send_hbm, send_out), (brick_hbm, brick_out),
+        (send_hbm, send_out), (brick_hbm, slot_ref),
     )
     copies = [pltpu.make_async_copy(a, b, sems.at[i]) for i, (a, b) in enumerate(pairs)]
     for copy in copies:
@@ -71,6 +71,11 @@
             out_ref[d, row:] = jnp.zeros((out_ref.shape[1] - row, LANES), jnp.float32)
     for copy in copies[4:]:
         copy.wait()
+    slot = slot_ref[...]
+    owner = jnp.zeros_like(slot)
+    for d in range(1, zones):
+        owner = owner + jnp.where(slot >= d * cap, 1, 0)
+    brick_out[...] = owner * out_ref.shape[1] + (slot - owner * cap) * (2 * SUBL)
 
 
 def stencil(v, table_ref, res_ref):
@@ -127,18 +132,17 @@
     subzones, entries = brick_ref.shape
     rows = 2 * subzones
     cap = out_ref.shape[2]
-    slots = out_ref.shape[0] * cap
+    pitch = data_ref.shape[0] // out_ref.shape[0]
     wave = wave_ref[0]
+    table = brick_ref[...]
+    starts = [[pl.multiple_of(table[s, k], SUBL) for k in range(entries)] for s in range(subzones)]
     grid = [(x, y) for x in range(entries) for y in range(SUBL)]
 
     def swap(v):
         return pltpu.roll(v, subzones, 0)
 
     def moduli(s, k):
-        q = brick_ref[s, k]
-        shear = data_ref[q // cap, pl.ds(pl.multiple_of(q % cap * 2 * SUBL, SUBL), SUBL)]
-        damping = data_ref[q // cap, pl.ds(pl.multiple_of((q % cap * 2 + 1) * SUBL, SUBL), SUBL)]
-        return shear, damping
+        return data_ref[pl.ds(starts[s][k], SUBL)], data_ref[pl.ds(starts[s][k] + SUBL, SUBL)]
 
     def rows_of(p, s, k):
         return pl.ds(k * SUBL * rows + p * subzones + s, SUBL, stride=rows)
@@ -205,17 +209,18 @@
             g_alpha, g_beta, g_gamma = real[0] + imag[0], real[1] + imag[1], real[2] - imag[2]
             mixed = damping * g_gamma - g_beta
             g_rate = wave * g_alpha + shear * mixed
-            q = brick_ref[s, k]
-            sum_ref[s, q, 0] += rate * (mixed - 6.0 * g_rate / diag)
-            sum_ref[s, q, 1] += rate * shear * g_gamma
-    for q in range(slots):
-        for p in range(2):
-            total = sum_ref[0, q, p]
-            for s in range(1, subzones):
-                total = total + sum_ref[s, q, p]
-            total = 2.0 * total
-            for y in range(out_ref.shape[1]):
-                out_ref[q // cap, y, q % cap, p] = total
+            sum_ref[s, pl.ds(starts[s][k], SUBL)] += rate * (mixed - 6.0 * g_rate / diag)
+            sum_ref[s, pl.ds(starts[s][k] + SUBL, SUBL)] += rate * shear * g_gamma
+    for o in range(out_ref.shape[0]):
+        for c in range(cap):
+            for p in range(2):
+                at = o * pitch + (2 * c + p) * SUBL
+                total = sum_ref[0, at : at + SUBL]
+                for s in range(1, subzones):
+                    total = total + sum_ref[s, at : at + SUBL]
+                total = 2.0 * total
+                for y in range(out_ref.shape[1]):
+                    out_ref[o, y, c, p] = total
 
 
 def update_kernel(
@@ -227,11 +232,12 @@
     lane = lax.broadcasted_iota(jnp.int32, (SUBL, LANES), 1)
     z_first = lane % BZ == 0
     z_last = lane % BZ == BZ - 1
+    table = send_ref[...]
     total_ref[...] = jnp.zeros_like(total_ref)
     use_ref[...] = jnp.zeros_like(use_ref)
     for d in range(zones):
         for c in range(cap):
-            local = send_ref[c, d]
+            local = table[c, d]
             local = jnp.where(local < 0, owned, local)
             got = total_ref[local]
             for y in range(mine_ref.shape[1]):
@@ -283,6 +289,7 @@
         scratch_shapes=[
             pltpu.SMEM((cap, zones), i32),
             pltpu.SMEM(brick_list.shape, i32),
+            pltpu.VMEM(brick_list.shape, i32),
             pltpu.VMEM((owned, 3, *cells), f32),
             pltpu.VMEM((owned, *cells), f32),
             pltpu.VMEM((owned, 2, *cells), f32),
@@ -308,7 +315,7 @@
     slots = pl.pallas_call(
         solve_kernel,
         out_shape=shape((zones, lines, cap, 2, *cells), f32),
-        in_specs=[SMEM, SMEM] + [VMEM] * 4,
+        in_specs=[VMEM, SMEM] + [VMEM] * 4,
         out_specs=VMEM,
         scratch_shapes=[
             pltpu.VMEM((3, sites, LANES), f32),
@@ -317,11 +324,11 @@
             pltpu.VMEM(state, f32),
             pltpu.VMEM((3, sites, LANES), f32),
             pltpu.VMEM((sites, 2 * LANES), f32),
-            pltpu.VMEM((subzones, zones * cap, 2, *cells), f32),
+            pltpu.VMEM((subzones, zones * rows, LANES), f32),
         ],
         compiler_params=room((8 * SWEEPS + 8) * seen.size + 2 * outgoing_size + (2 + subzones) * slot_size),
         name="solve",
-    )(bricks, wave_sq, arrived, start, sten0, neighbours)
+    )(bricks, wave_sq, arrived.reshape(zones * rows, LANES), start, sten0, neighbours)
     slots = slots.reshape(zones * lines, cap, 2, *cells)
     mine = lax.all_to_all(slots, ("zone", "line"), split_axis=0, concat_axis=0, tiled=True)
     if cores == 2:
@@ -333,7 +340,7 @@
     results = pl.pallas_call(
         functools.partial(update_kernel, float(lines * cores)),
         out_shape=(whole, whole, whole),
-        in_specs=[SMEM] + [VMEM] * 7,
+        in_specs=[VMEM] * 8,
         out_specs=(VMEM, VMEM, VMEM),
         scratch_shapes=[
             pltpu.VMEM((owned + 1, 2, *cells), f32),

time: 36.9 us -> 35.9 us (0.973)
  Pallas kernels: 6.43 us -> 5.44 us
    pallas_call x1, Pallas kernels: 2.75 us -> 2.22 us  [on_device(): pl.pallas_call(solve_kernel, out_shape=shape((zones, lines, cap, 2, *cell...]
    pallas_call x1, Pallas kernels: 1.45 us -> 0.99 us  [on_device(): pl.pallas_call(functools.partial(update_kernel, float(lines * cores)), ou...]
where the time goes in v4:
time: 35.9 us; the launch traced here: 35.6 us
  blocking collectives  13.4 us (37%)
  waiting for transfers between devices  8 us (22%)
  starting transfers between devices  7.3 us (20%)
  Pallas kernels  5.44 us (15%)
  between operations  1.37 us (4%)
    all_to_all x1, blocking collectives, on_device(): lax.all_to_all(slots, ('zone', 'line'), split_axis=0, concat_axis=0, tile...  13.4 us
    all_to_all x1, starting transfers between devices, on_device(): lax.all_to_all(outgoing, 'zone', split_axis=0, concat_axis=0, tiled=True)  7.29 us
    all_to_all x1, waiting for transfers between devices, on_device(): lax.all_to_all(outgoing, 'zone', split_axis=0, concat_axis=0, tiled=True)  6.47 us
    pallas_call x1, Pallas kernels, on_device(): pl.pallas_call(solve_kernel, out_shape=shape((zones, lines, cap, 2, *cell...  2.22 us
    pallas_call x1, Pallas kernels, on_device(): pl.pallas_call(pack_kernel, out_shape=(shape((zones, rows, LANES), f32),...  1.8 us
    ppermute x1, waiting for transfers between devices, on_device(): other = lax.ppermute(mine, 'core', [(0, 1), (1, 0)])  1.53 us
    pallas_call x1, Pallas kernels, on_device(): pl.pallas_call(functools.partial(update_kernel, float(lines * cores)), ou...  0.99 us
  transfers between devices with their start and end apart: 2, of which 2 were waited for; matrix products, arithmetic and copies ran while one was open for 0% of the time, Pallas kernels for 1%

profile of v4, /device:TPU:0, one launch (start us, length us, event | category | flops | bytes accessed | tf_op | source)
XLA Modules:
  0.0 35.6 jit_solution(2660217427383868505)
XLA Ops:
  0.6 0.0 copy-start.1
  0.6 1.8 %pack.1 = (f32[8,40,128]{2,1,0:T(8,128)}, s32[2,8]{1,0:T(2,128)S(1)}, s32[4,8]{1,0:T(4,128)S(1)}) custom-call(s32[2,8]{1,0:T(2,128)} %bitcast.30, s32[4,8]{1,0:T(4,128)} %brick_hbm.1, f32[8,3,8,128]{3,2,1,0:T(8,128)} %bitcast.22, f32[8,8,128]{2,1,0:T(8,128)} %bitcast.26), custom_call_target="tpu_custom_call" | custom-call | tf_op jit(solution)/shard_map/pack/pallas_call | solution.py:282
  2.4 7.3 %all-to-all-start = ((f32[8,40,128]{2,1,0:T(8,128)}), f32[8,40,128]{2,1,0:T(8,128)S(1)}, u32[]{:S(2)}, u32[]{:S(2)}) async-start(f32[8,40,128]{2,1,0:T(8,128)} %get-tuple-element.14), calls=%async_computation | async-start | bytes 327680 | tf_op jit(solution)/shard_map/all_to_all | solution.py:301
  10.4 0.0 copy-done.1
  10.4 0.4 %prepare.1 = (f32[8,8,8,128]{3,2,1,0:T(8,128)S(1)}, f32[8,8,8,128]{3,2,1,0:T(8,128)S(1)}, bf16[256,256]{1,0:T(8,128)(2,1)S(1)}) custom-call(f32[512,128]{1,0:T(8,128)S(1)} %bitcast.25), custom_call_target="tpu_custom_call" | custom-call | flops 16777216 | bytes 1048576 | tf_op jit(solution)/shard_map/prepare/pallas_call | solution.py:305
  10.8 6.5 %all-to-all-done.data_ref = f32[8,40,128]{2,1,0:T(8,128)S(1)} async-done(((f32[8,40,128]{2,1,0:T(8,128)}), f32[8,40,128]{2,1,0:T(8,128)S(1)}, u32[]{:S(2)}, u32[]{:S(2)}) %all-to-all-start) | async-done | bytes 163872 | tf_op jit(solution)/shard_map/all_to_all | solution.py:301
  17.3 2.2 %solve.1 = f32[8,2,2,2,8,128]{5,4,3,2,1,0:T(8,128)S(1)} custom-call(s32[4,8]{1,0:T(4,128)S(1)} %get-tuple-element.13.brick_ref, f32[1]{0:T(128)S(6)} %copy.26.wave_ref, f32[320,128]{1,0:T(8,128)S(1)} %bitcast.19, f32[8,8,8,128]{3,2,1,0:T(8,128)S(1)} %get-tuple-element.15.start_ref, f32[8,8,8,128]{3,2,1,0:T(8,128)S(1)} %get-tuple-element.16.sten0_ref, ...), custom_call_target="tpu_custom_call" | custom-call | tf_op jit(solution)/shard_map/solve/pallas_call | solution.py:315
  19.5 0.0 copy-start
  19.5 0.0 copy-start.2
  19.6 0.0 copy-start.3
  19.6 0.0 copy-start.4
  19.6 13.4 %all_to_all.10 = f32[16,2,2,8,128]{4,3,2,1,0:T(8,128)S(1)} all-to-all(f32[16,2,2,8,128]{4,3,2,1,0:T(8,128)S(1)} %bitcast.21), channel_id=1, replica_groups=mesh['zone'=8,'line'=2,'core'=2] {'zone','line'}, dimensions={0} | all-to-all | bytes 524288 | tf_op jit(solution)/shard_map/all_to_all | solution.py:333
  33.0 0.0 collective-permute-start
  33.0 1.5 %collective-permute-done = f32[16,2,2,8,128]{4,3,2,1,0:T(8,128)S(1)} collective-permute-done((f32[16,2,2,8,128]{4,3,2,1,0:T(8,128)S(1)}, f32[16,2,2,8,128]{4,3,2,1,0:T(8,128)S(1)}, u32[]{:S(2)}, u32[]{:S(2)}) %collective-permute-start) | collective-permute-done | bytes 262176 | tf_op jit(solution)/shard_map/ppermute | solution.py:335
  34.6 0.0 copy-done
  34.6 0.0 copy-done.2
  34.6 0.0 copy-done.3
  34.6 0.0 copy-done.4
  34.6 1.0 %update.1 = (f32[8,3,8,128]{3,2,1,0:T(8,128)}, f32[8,3,8,128]{3,2,1,0:T(8,128)}, f32[8,3,8,128]{3,2,1,0:T(8,128)}) custom-call(s32[2,8]{1,0:T(2,128)S(1)} %get-tuple-element.12.send_ref, f32[8,2,2,2,8,128]{5,4,3,2,1,0:T(8,128)S(1)} %bitcast.20, f32[8,2,2,2,8,128]{5,4,3,2,1,0:T(8,128)S(1)} %bitcast.24, f32[8,40,128]{2,1,0:T(8,128)S(1)} %all-to-all-done.data_ref, ...), custom_call_target="tpu_custom_call" | custom-call | tf_op jit(solution)/shard_map/update/pallas_call | solution.py:340
Async XLA Ops:
  0.6 9.8 %copy-start.1 = (f32[1,4,2,8,1024]{4,3,2,1,0:T(8,128)S(1)}, f32[1,4,2,8,1024]{4,3,2,1,0:T(8,128)}, u32[]{:S(2)}) copy-start(f32[1,4,2,8,1024]{4,3,2,1,0:T(8,128)} %param.12) | copy-start | bytes 786436
  2.4 14.9 %all-to-all-start = ((f32[8,40,128]{2,1,0:T(8,128)}), f32[8,40,128]{2,1,0:T(8,128)S(1)}, u32[]{:S(2)}, u32[]{:S(2)}) async-start(f32[8,40,128]{2,1,0:T(8,128)} %get-tuple-element.14), calls=%async_computation | async-start | bytes 327680 | tf_op jit(solution)/shard_map/all_to_all | solution.py:301
  19.5 15.0 %copy-start = (f32[8,3,1,1024]{3,2,1,0:T(1,128)S(1)}, f32[8,3,1,1024]{3,2,1,0:T(1,128)}, u32[]{:S(2)}) copy-start(f32[8,3,1,1024]{3,2,1,0:T(1,128)} %param.8) | copy-start | bytes 294916
  19.5 15.0 %copy-start.2 = (f32[8,1,1024]{2,1,0:T(1,128)S(1)}, f32[8,1,1024]{2,1,0:T(1,128)}, u32[]{:S(2)}) copy-start(f32[8,1,1024]{2,1,0:T(1,128)} %param.11) | copy-start | bytes 98308
  19.6 15.0 %copy-start.3 = (f32[8,3,1,1024]{3,2,1,0:T(1,128)S(1)}, f32[8,3,1,1024]{3,2,1,0:T(1,128)}, u32[]{:S(2)}) copy-start(f32[8,3,1,1024]{3,2,1,0:T(1,128)} %param.9) | copy-start | bytes 294916
  19.6 15.0 %copy-start.4 = (f32[8,3,1,1024]{3,2,1,0:T(1,128)S(1)}, f32[8,3,1,1024]{3,2,1,0:T(1,128)}, u32[]{:S(2)}) copy-start(f32[8,3,1,1024]{3,2,1,0:T(1,128)} %param.10) | copy-start | bytes 294916
  33.0 1.5 %collective-permute-start = (f32[16,2,2,8,128]{4,3,2,1,0:T(8,128)S(1)}, f32[16,2,2,8,128]{4,3,2,1,0:T(8,128)S(1)}, u32[]{:S(2)}, u32[]{:S(2)}) collective-permute-start(f32[16,2,2,8,128]{4,3,2,1,0:T(8,128)S(1)} %all_to_all.10), channel_id=1, source_target_pairs={{0,1},{1,0},{2,3},{3,2},{4,5},{5,4},{6,7},{7,6},{8,9},{9,8},{10,11... | collective-permute-start | bytes 786440 | tf_op jit(solution)/shard_map/ppermute | solution.py:335

commit v5 on v4

--- a/solution.py
+++ b/solution.py
@@ -44,6 +44,7 @@
     for copy in copies[:4]:
         copy.wait()
     cap, zones = send_ref.shape
+    pitch = out_ref.shape[0] // zones
     owned = modulus_ref.shape[0]
     for b in range(owned):
         fib = fiber_ref[b]
@@ -58,24 +59,24 @@
                 uses = uses + jnp.where(slot_at == brick_ref[s, k] - first, 1.0, 0.0)
         for q in range(first, min(first + LANES, zones * cap)):
             wide = jnp.broadcast_to(uses[:1, q - first : q - first + 1], (1, LANES))
-            row = 2 * SUBL * cap + q % cap
-            out_ref[q // cap, row : row + 1] = wide
+            row = q // cap * pitch + 2 * SUBL * cap + q % cap
+            out_ref[row : row + 1] = wide
     for d in range(zones):
         for c in range(cap):
             local = jnp.maximum(send_ref[c, d], 0)
             for p in range(2):
-                row = (2 * c + p) * SUBL
-                out_ref[d, row : row + SUBL] = plane_ref[local, p]
+                row = d * pitch + (2 * c + p) * SUBL
+                out_ref[row : row + SUBL] = plane_ref[local, p]
         row = 2 * SUBL * cap + cap
-        if row < out_ref.shape[1]:
-            out_ref[d, row:] = jnp.zeros((out_ref.shape[1] - row, LANES), jnp.float32)
+        if row < pitch:
+            out_ref[d * pitch + row : (d + 1) * pitch] = jnp.zeros((pitch - row, LANES), jnp.float32)
     for copy in copies[4:]:
         copy.wait()
     slot = slot_ref[...]
     owner = jnp.zeros_like(slot)
     for d in range(1, zones):
         owner = owner + jnp.where(slot >= d * cap, 1, 0)
-    brick_out[...] = owner * out_ref.shape[1] + (slot - owner * cap) * (2 * SUBL)
+    brick_out[...] = owner * pitch + (slot - owner * cap) * (2 * SUBL)
 
 
 def stencil(v, table_ref, res_ref):
@@ -126,13 +127,14 @@
 
 
 def solve_kernel(
-    brick_ref, wave_ref, data_ref, start_ref, sten0_ref, table_ref, out_ref,
+    brick_ref, wave_ref, data_ref, start_ref, sten0_ref, table_ref, keep_ref, give_ref,
     coef_ref, field_ref, sten_ref, lam_ref, grad_ref, res_ref, sum_ref,
 ):
     subzones, entries = brick_ref.shape
     rows = 2 * subzones
-    cap = out_ref.shape[2]
-    pitch = data_ref.shape[0] // out_ref.shape[0]
+    zones, cap = keep_ref.shape[:2]
+    pitch = data_ref.shape[0] // zones
+    core = lax.axis_index("core")
     wave = wave_ref[0]
     table = brick_ref[...]
     starts = [[pl.multiple_of(table[s, k], SUBL) for k in range(entries)] for s in range(subzones)]
@@ -211,16 +213,21 @@
             g_rate = wave * g_alpha + shear * mixed
             sum_ref[s, pl.ds(starts[s][k], SUBL)] += rate * (mixed - 6.0 * g_rate / diag)
             sum_ref[s, pl.ds(starts[s][k] + SUBL, SUBL)] += rate * shear * g_gamma
-    for o in range(out_ref.shape[0]):
-        for c in range(cap):
-            for p in range(2):
-                at = o * pitch + (2 * c + p) * SUBL
-                total = sum_ref[0, at : at + SUBL]
+    for out_ref, half in ((keep_ref, core), (give_ref, 1 - core)):
+        first = pl.multiple_of(half * (cap * SUBL), SUBL)
+        for o in range(zones):
+            for j in range(cap):
+                at = pl.ds(first + (o * pitch + j * SUBL), SUBL)
+                total = sum_ref[0, at]
                 for s in range(1, subzones):
-                    total = total + sum_ref[s, at : at + SUBL]
-                total = 2.0 * total
-                for y in range(out_ref.shape[1]):
-                    out_ref[o, y, c, p] = total
+                    total = total + sum_ref[s, at]
+                out_ref[o, j] = 2.0 * total
+
+
+def join_kernel(keep_ref, given_ref, out_ref):
+    total = keep_ref[...] + given_ref[...]
+    for y in range(out_ref.shape[1]):
+        out_ref[:, y] = total
 
 
 def update_kernel(
@@ -235,15 +242,23 @@
     table = send_ref[...]
     total_ref[...] = jnp.zeros_like(total_ref)
     use_ref[...] = jnp.zeros_like(use_ref)
+    lower = lax.axis_index("core") == 0
+    pitch = data_ref.shape[0] // zones
     for d in range(zones):
+        units = [[], []]
+        for j in range(cap):
+            own, got = mine_ref[d, 0, j], other_ref[d, 0, j]
+            for y in range(1, mine_ref.shape[1]):
+                own, got = own + mine_ref[d, y, j], got + other_ref[d, y, j]
+            units[0].append(jnp.where(lower, own, got))
+            units[1].append(jnp.where(lower, got, own))
+        units = units[0] + units[1]
         for c in range(cap):
             local = table[c, d]
             local = jnp.where(local < 0, owned, local)
-            got = total_ref[local]
-            for y in range(mine_ref.shape[1]):
-                got = got + (mine_ref[d, y, c] + other_ref[d, y, c])
-            total_ref[local] = got
-            use_ref[local] += data_ref[d, pl.ds(2 * SUBL * cap + c, 1)]
+            for p in range(2):
+                total_ref[local, p] += units[2 * c + p]
+            use_ref[local] += data_ref[pl.ds(d * pitch + 2 * SUBL * cap + c, 1)]
     for b in range(owned):
         fib = fiber_ref[b]
         fib_sq = fib * fib
@@ -282,7 +297,7 @@
     outgoing, send_table, bricks = pl.pallas_call(
         pack_kernel,
         out_shape=(
-            shape((zones, rows, LANES), f32), shape((cap, zones), i32), shape(brick_list.shape, i32),
+            shape((zones * rows, LANES), f32), shape((cap, zones), i32), shape(brick_list.shape, i32),
         ),
         in_specs=[HBM] * 4,
         out_specs=(VMEM,) * 3,
@@ -312,11 +327,12 @@
         cost_estimate=pl.CostEstimate(flops=2**24, bytes_accessed=16 * seen.size, transcendentals=0),
         name="prepare",
     )(seen)
-    slots = pl.pallas_call(
+    half = shape((zones, cap, *cells), f32)
+    keep, give = pl.pallas_call(
         solve_kernel,
-        out_shape=shape((zones, lines, cap, 2, *cells), f32),
+        out_shape=(half, half),
         in_specs=[VMEM, SMEM] + [VMEM] * 4,
-        out_specs=VMEM,
+        out_specs=(VMEM, VMEM),
         scratch_shapes=[
             pltpu.VMEM((3, sites, LANES), f32),
             pltpu.VMEM((SWEEPS - 1, *state), f32),
@@ -328,14 +344,20 @@
         ],
         compiler_params=room((8 * SWEEPS + 8) * seen.size + 2 * outgoing_size + (2 + subzones) * slot_size),
         name="solve",
-    )(bricks, wave_sq, arrived.reshape(zones * rows, LANES), start, sten0, neighbours)
-    slots = slots.reshape(zones * lines, cap, 2, *cells)
+    )(bricks, wave_sq, arrived, start, sten0, neighbours)
+    other_core = [(0, 1), (1, 0)]
+    slots = pl.pallas_call(
+        join_kernel,
+        out_shape=shape((zones, lines, cap, *cells), f32),
+        in_specs=[VMEM, VMEM],
+        out_specs=VMEM,
+        compiler_params=room(2 * slot_size),
+        name="join",
+    )(keep, lax.ppermute(give, "core", other_core))
+    slots = slots.reshape(zones * lines, cap, *cells)
     mine = lax.all_to_all(slots, ("zone", "line"), split_axis=0, concat_axis=0, tiled=True)
-    if cores == 2:
-        other = lax.ppermute(mine, "core", [(0, 1), (1, 0)])
-    else:
-        other = jnp.zeros_like(mine)
-    mine, other = (a.reshape(zones, lines, cap, 2, *cells) for a in (mine, other))
+    other = lax.ppermute(mine, "core", other_core)
+    mine, other = (a.reshape(zones, lines, cap, *cells) for a in (mine, other))
     whole = jax.ShapeDtypeStruct((owned, 3, *cells), f32)
     results = pl.pallas_call(
         functools.partial(update_kernel, float(lines * cores)),

time: 35.9 us -> 35.2 us (0.981)
  blocking collectives: 13.4 us -> 11.6 us
  waiting for transfers between devices: 8 us -> 9.05 us
    all_to_all x1, blocking collectives: 13.4 us -> 11.6 us  [on_device(): lax.all_to_all(slots, ('zone', 'line'), split_axis=0, concat_axis=0, tile...]
    ppermute x1 -> x2, waiting for transfers between devices: 1.53 us -> 2.59 us  [the longest x1 1.35 us: on_device(): other = lax.ppermute(mine, 'core', other_core)]
    pallas_call x2 -> x3, Pallas kernels: 4.02 us -> 4.04 us  [the longest x1 2.22 us: on_device(): pl.pallas_call(solve_kernel, out_shape=(half, half), in_specs=[VMEM, SMEM...]
  transfers between devices with their start and end apart: 2 -> 3, of which waited for: 2 -> 3; matrix products, arithmetic and copies ran while one was open for 0% -> 0% of each run, Pallas kernels for 1% -> 1%
where the time goes in v5:
time: 35.2 us; the launch traced here: 34.9 us
  blocking collectives  11.6 us (33%)
  waiting for transfers between devices  9.05 us (26%)
  starting transfers between devices  7.37 us (21%)
  Pallas kernels  5.45 us (15%)
  between operations  1.37 us (4%)
    all_to_all x1, blocking collectives, on_device(): lax.all_to_all(slots, ('zone', 'line'), split_axis=0, concat_axis=0, tile...  11.6 us
    all_to_all x1, starting transfers between devices, on_device(): lax.all_to_all(outgoing, 'zone', split_axis=0, concat_axis=0, tiled=True)  7.29 us
    all_to_all x1, waiting for transfers between devices, on_device(): lax.all_to_all(outgoing, 'zone', split_axis=0, concat_axis=0, tiled=True)  6.47 us
    pallas_call x1, Pallas kernels, on_device(): pl.pallas_call(solve_kernel, out_shape=(half, half), in_specs=[VMEM, SMEM...  2.22 us
    pallas_call x1, Pallas kernels, on_device(): pl.pallas_call(pack_kernel, out_shape=(shape((zones * rows, LANES), f32),...  1.81 us
    ppermute x1, waiting for transfers between devices, on_device(): other = lax.ppermute(mine, 'core', other_core)  1.35 us
    ppermute x1, waiting for transfers between devices, on_device(): lax.ppermute(give, 'core', other_core)  1.24 us
    pallas_call x1, Pallas kernels, on_device(): pl.pallas_call(functools.partial(update_kernel, float(lines * cores)), ou...  0.98 us
  transfers between devices with their start and end apart: 3, of which 3 were waited for; matrix products, arithmetic and copies ran while one was open for 0% of the time, Pallas kernels for 1%

profile of v5, /device:TPU:0, one launch (start us, length us, event | category | flops | bytes accessed | tf_op | source)
XLA Modules:
  0.0 34.9 jit_solution(16126961491737129033)
XLA Ops:
  0.6 0.0 copy-start.1
  0.6 1.8 %pack.1 = (f32[320,128]{1,0:T(8,128)}, s32[2,8]{1,0:T(2,128)S(1)}, s32[4,8]{1,0:T(4,128)S(1)}) custom-call(s32[2,8]{1,0:T(2,128)} %bitcast.32, s32[4,8]{1,0:T(4,128)} %brick_hbm.1, f32[8,3,8,128]{3,2,1,0:T(8,128)} %bitcast.24, f32[8,8,128]{2,1,0:T(8,128)} %bitcast.27), custom_call_target="tpu_custom_call" | custom-call | tf_op jit(solution)/shard_map/pack/pallas_call | solution.py:297
  2.5 7.3 %all-to-all-start = ((f32[8,40,128]{2,1,0:T(8,128)}), f32[8,40,128]{2,1,0:T(8,128)S(1)}, u32[]{:S(2)}, u32[]{:S(2)}) async-start(f32[8,40,128]{2,1,0:T(8,128)} %bitcast.4), calls=%async_computation | async-start | bytes 327680 | tf_op jit(solution)/shard_map/all_to_all | solution.py:316
  10.4 0.0 copy-done.1
  10.4 0.4 %prepare.1 = (f32[8,8,8,128]{3,2,1,0:T(8,128)S(1)}, f32[8,8,8,128]{3,2,1,0:T(8,128)S(1)}, bf16[256,256]{1,0:T(8,128)(2,1)S(1)}) custom-call(f32[512,128]{1,0:T(8,128)S(1)} %bitcast.26), custom_call_target="tpu_custom_call" | custom-call | flops 16777216 | bytes 1048576 | tf_op jit(solution)/shard_map/prepare/pallas_call | solution.py:320
  10.8 6.5 %all-to-all-done = f32[8,40,128]{2,1,0:T(8,128)S(1)} async-done(((f32[8,40,128]{2,1,0:T(8,128)}), f32[8,40,128]{2,1,0:T(8,128)S(1)}, u32[]{:S(2)}, u32[]{:S(2)}) %all-to-all-start) | async-done | bytes 163872 | tf_op jit(solution)/shard_map/all_to_all | solution.py:316
  17.3 2.2 %solve.1 = (f32[8,2,8,128]{3,2,1,0:T(8,128)S(1)}, f32[8,2,8,128]{3,2,1,0:T(8,128)S(1)}) custom-call(s32[4,8]{1,0:T(4,128)S(1)} %get-tuple-element.15.brick_ref, f32[1]{0:T(128)S(6)} %copy.26.wave_ref, f32[320,128]{1,0:T(8,128)S(1)} %bitcast.20, f32[8,8,8,128]{3,2,1,0:T(8,128)S(1)} %get-tuple-element.17.start_ref, ...), custom_call_target="tpu_custom_call" | custom-call | tf_op jit(solution)/shard_map/solve/pallas_call | solution.py:331
  19.5 0.1 collective-permute-start
  19.6 1.2 %collective-permute-done.given_ref = f32[8,2,8,128]{3,2,1,0:T(8,128)S(1)} collective-permute-done((f32[8,2,8,128]{3,2,1,0:T(8,128)S(1)}, f32[8,2,8,128]{3,2,1,0:T(8,128)S(1)}, u32[]{:S(2)}, u32[]{:S(2)}) %collective-permute-start) | collective-permute-done | bytes 65568 | tf_op jit(solution)/shard_map/ppermute | solution.py:356
  20.9 0.0 copy-start.4
  20.9 0.0 copy-start
  20.9 0.0 copy-start.2
  20.9 0.0 copy-start.3
  20.9 11.6 %all_to_all.16 = f32[16,2,8,128]{3,2,1,0:T(8,128)S(1)} all-to-all(f32[16,2,8,128]{3,2,1,0:T(8,128)S(1)} %bitcast.22), channel_id=1, replica_groups=mesh['zone'=8,'line'=2,'core'=2] {'zone','line'}, dimensions={0} | all-to-all | bytes 262144 | tf_op jit(solution)/shard_map/all_to_all | solution.py:358
  32.5 0.0 collective-permute-start.1
  32.6 1.3 %collective-permute-done.1 = f32[16,2,8,128]{3,2,1,0:T(8,128)S(1)} collective-permute-done((f32[16,2,8,128]{3,2,1,0:T(8,128)S(1)}, f32[16,2,8,128]{3,2,1,0:T(8,128)S(1)}, u32[]{:S(2)}, u32[]{:S(2)}) %collective-permute-start.1) | collective-permute-done | bytes 131104 | tf_op jit(solution)/shard_map/ppermute | solution.py:359
  33.9 0.0 copy-done.4
  33.9 0.0 copy-done
  33.9 0.0 copy-done.2
  33.9 0.0 copy-done.3
  33.9 1.0 %update.1 = (f32[8,3,8,128]{3,2,1,0:T(8,128)}, f32[8,3,8,128]{3,2,1,0:T(8,128)}, f32[8,3,8,128]{3,2,1,0:T(8,128)}) custom-call(s32[2,8]{1,0:T(2,128)S(1)} %get-tuple-element.14.send_ref, f32[8,2,2,8,128]{4,3,2,1,0:T(8,128)S(1)} %bitcast.23, f32[8,2,2,8,128]{4,3,2,1,0:T(8,128)S(1)} %bitcast.29, f32[320,128]{1,0:T(8,128)S(1)} %bitcast.21, ...), custom_call_target="tpu_custom_call" | custom-call | tf_op jit(solution)/shard_map/update/pallas_call | solution.py:362
  (1 shorter events, 0.0 us)
Async XLA Ops:
  0.6 9.8 %copy-start.1 = (f32[1,4,2,8,1024]{4,3,2,1,0:T(8,128)S(1)}, f32[1,4,2,8,1024]{4,3,2,1,0:T(8,128)}, u32[]{:S(2)}) copy-start(f32[1,4,2,8,1024]{4,3,2,1,0:T(8,128)} %param.12) | copy-start | bytes 786436
  2.5 14.9 %all-to-all-start = ((f32[8,40,128]{2,1,0:T(8,128)}), f32[8,40,128]{2,1,0:T(8,128)S(1)}, u32[]{:S(2)}, u32[]{:S(2)}) async-start(f32[8,40,128]{2,1,0:T(8,128)} %bitcast.4), calls=%async_computation | async-start | bytes 327680 | tf_op jit(solution)/shard_map/all_to_all | solution.py:316
  19.5 1.3 %collective-permute-start = (f32[8,2,8,128]{3,2,1,0:T(8,128)S(1)}, f32[8,2,8,128]{3,2,1,0:T(8,128)S(1)}, u32[]{:S(2)}, u32[]{:S(2)}) collective-permute-start(f32[8,2,8,128]{3,2,1,0:T(8,128)S(1)} %get-tuple-element.21), channel_id=1, source_target_pairs={{0,1},{1,0},{2,3},{3,2},{4,5},{5,4},{6,7},{7,6},{8,9},{9,8},{10,11... | collective-permute-start | bytes 196616 | tf_op jit(solution)/shard_map/ppermute | solution.py:356
  20.9 13.0 %copy-start.4 = (f32[8,3,1,1024]{3,2,1,0:T(1,128)S(1)}, f32[8,3,1,1024]{3,2,1,0:T(1,128)}, u32[]{:S(2)}) copy-start(f32[8,3,1,1024]{3,2,1,0:T(1,128)} %param.10) | copy-start | bytes 294916
  20.9 13.0 %copy-start = (f32[8,3,1,1024]{3,2,1,0:T(1,128)S(1)}, f32[8,3,1,1024]{3,2,1,0:T(1,128)}, u32[]{:S(2)}) copy-start(f32[8,3,1,1024]{3,2,1,0:T(1,128)} %param.8) | copy-start | bytes 294916
  20.9 13.0 %copy-start.2 = (f32[8,1,1024]{2,1,0:T(1,128)S(1)}, f32[8,1,1024]{2,1,0:T(1,128)}, u32[]{:S(2)}) copy-start(f32[8,1,1024]{2,1,0:T(1,128)} %param.11) | copy-start | bytes 98308
  20.9 13.0 %copy-start.3 = (f32[8,3,1,1024]{3,2,1,0:T(1,128)S(1)}, f32[8,3,1,1024]{3,2,1,0:T(1,128)}, u32[]{:S(2)}) copy-start(f32[8,3,1,1024]{3,2,1,0:T(1,128)} %param.9) | copy-start | bytes 294916
  32.5 1.3 %collective-permute-start.1 = (f32[16,2,8,128]{3,2,1,0:T(8,128)S(1)}, f32[16,2,8,128]{3,2,1,0:T(8,128)S(1)}, u32[]{:S(2)}, u32[]{:S(2)}) collective-permute-start(f32[16,2,8,128]{3,2,1,0:T(8,128)S(1)} %all_to_all.16), channel_id=1, source_target_pairs={{0,1},{1,0},{2,3},{3,2},{4,5},{5,4},{6,7},{7,6},{8,9},{9,8},{10,11... | collective-permute-start | bytes 393224 | tf_op jit(solution)/shard_map/ppermute | solution.py:359

commit v6 on v5

--- a/solution.py
+++ b/solution.py
@@ -67,16 +67,15 @@
             for p in range(2):
                 row = d * pitch + (2 * c + p) * SUBL
                 out_ref[row : row + SUBL] = plane_ref[local, p]
-        row = 2 * SUBL * cap + cap
-        if row < pitch:
-            out_ref[d * pitch + row : (d + 1) * pitch] = jnp.zeros((pitch - row, LANES), jnp.float32)
     for copy in copies[4:]:
         copy.wait()
     slot = slot_ref[...]
     owner = jnp.zeros_like(slot)
     for d in range(1, zones):
         owner = owner + jnp.where(slot >= d * cap, 1, 0)
-    brick_out[...] = owner * pitch + (slot - owner * cap) * (2 * SUBL)
+    subzones = slot.shape[0]
+    brick_out[:subzones] = owner * pitch + (slot - owner * cap) * (2 * SUBL)
+    brick_out[subzones:] = slot * (2 * SUBL)
 
 
 def stencil(v, table_ref, res_ref):
@@ -130,14 +129,14 @@
     brick_ref, wave_ref, data_ref, start_ref, sten0_ref, table_ref, keep_ref, give_ref,
     coef_ref, field_ref, sten_ref, lam_ref, grad_ref, res_ref, sum_ref,
 ):
-    subzones, entries = brick_ref.shape
+    subzones, entries = brick_ref.shape[0] // 2, brick_ref.shape[1]
     rows = 2 * subzones
     zones, cap = keep_ref.shape[:2]
-    pitch = data_ref.shape[0] // zones
     core = lax.axis_index("core")
     wave = wave_ref[0]
     table = brick_ref[...]
-    starts = [[pl.multiple_of(table[s, k], SUBL) for k in range(entries)] for s in range(subzones)]
+    starts = [[table[s, k] for k in range(entries)] for s in range(subzones)]
+    slots = [[pl.multiple_of(table[subzones + s, k], SUBL) for k in range(entries)] for s in range(subzones)]
     grid = [(x, y) for x in range(entries) for y in range(SUBL)]
 
     def swap(v):
@@ -211,13 +210,13 @@
             g_alpha, g_beta, g_gamma = real[0] + imag[0], real[1] + imag[1], real[2] - imag[2]
             mixed = damping * g_gamma - g_beta
             g_rate = wave * g_alpha + shear * mixed
-            sum_ref[s, pl.ds(starts[s][k], SUBL)] += rate * (mixed - 6.0 * g_rate / diag)
-            sum_ref[s, pl.ds(starts[s][k] + SUBL, SUBL)] += rate * shear * g_gamma
+            sum_ref[s, pl.ds(slots[s][k], SUBL)] += rate * (mixed - 6.0 * g_rate / diag)
+            sum_ref[s, pl.ds(slots[s][k] + SUBL, SUBL)] += rate * shear * g_gamma
     for out_ref, half in ((keep_ref, core), (give_ref, 1 - core)):
         first = pl.multiple_of(half * (cap * SUBL), SUBL)
         for o in range(zones):
             for j in range(cap):
-                at = pl.ds(first + (o * pitch + j * SUBL), SUBL)
+                at = pl.ds(first + (o * 2 * cap + j) * SUBL, SUBL)
                 total = sum_ref[0, at]
                 for s in range(1, subzones):
                     total = total + sum_ref[s, at]
@@ -236,6 +235,7 @@
 ):
     cap, zones = send_ref.shape
     owned = modulus_ref.shape[0]
+    lots = total_ref.shape[0]
     lane = lax.broadcasted_iota(jnp.int32, (SUBL, LANES), 1)
     z_first = lane % BZ == 0
     z_last = lane % BZ == BZ - 1
@@ -256,14 +256,16 @@
         for c in range(cap):
             local = table[c, d]
             local = jnp.where(local < 0, owned, local)
+            lot = d % lots
             for p in range(2):
-                total_ref[local, p] += units[2 * c + p]
-            use_ref[local] += data_ref[pl.ds(d * pitch + 2 * SUBL * cap + c, 1)]
+                total_ref[lot, c, local, p] += units[2 * c + p]
+            use_ref[lot, c, local] += data_ref[pl.ds(d * pitch + 2 * SUBL * cap + c, 1)]
     for b in range(owned):
         fib = fiber_ref[b]
         fib_sq = fib * fib
-        g_shear, g_damping = total_ref[b, 0], total_ref[b, 1]
-        share = 1.0 / (freq_count * jnp.maximum(use_ref[b], 1.0))
+        g_shear, g_damping = (sum(total_ref[i, c, b, p] for i in range(lots) for c in range(cap)) for p in range(2))
+        uses = sum(use_ref[i, c, b] for i in range(lots) for c in range(cap))
+        share = 1.0 / (freq_count * jnp.maximum(uses, 1.0))
         for p, grad in enumerate((g_shear * (1.0 - fib_sq), g_shear * fib_sq, g_damping)):
             descent = grad * share
             new_first = beta_first * first_ref[b, p] + (1.0 - beta_first) * descent
@@ -289,7 +291,7 @@
     fib = fiber.reshape(owned, *cells)
     seen = measured.reshape(subzones, 2, K, SUBL, LANES).swapaxes(2, 3).reshape(-1, LANES)
     f32 = jnp.float32
-    rows = 2 * SUBL * cap + -(-cap // SUBL) * SUBL
+    rows = 2 * SUBL * cap + cap
     outgoing_size = zones * rows * LANES
     slot_size = zones * lines * cap * 2 * SUBL * LANES
     i32 = jnp.int32
@@ -297,7 +299,7 @@
     outgoing, send_table, bricks = pl.pallas_call(
         pack_kernel,
         out_shape=(
-            shape((zones * rows, LANES), f32), shape((cap, zones), i32), shape(brick_list.shape, i32),
+            shape((zones * rows, LANES), f32), shape((cap, zones), i32), shape((2 * subzones, K), i32),
         ),
         in_specs=[HBM] * 4,
         out_specs=(VMEM,) * 3,
@@ -313,7 +315,8 @@
         compiler_params=room(outgoing_size + 4 * modulus.size),
         name="pack",
     )(*(pltpu.with_memory_space_constraint(a, pltpu.HBM) for a in (send_list[0].T, brick_list, mod, fib)))
-    arrived = lax.all_to_all(outgoing, "zone", split_axis=0, concat_axis=0, tiled=True)
+    outgoing = outgoing.reshape(zones * rows, 1, LANES)
+    arrived = lax.all_to_all(outgoing, "zone", split_axis=0, concat_axis=0, tiled=True).reshape(zones * rows, LANES)
     state = (K, SUBL, 2 * subzones, LANES)
     sites = K * SUBL * 2 * subzones
     table = (2 * LANES, 2 * LANES)
@@ -340,7 +343,7 @@
             pltpu.VMEM(state, f32),
             pltpu.VMEM((3, sites, LANES), f32),
             pltpu.VMEM((sites, 2 * LANES), f32),
-            pltpu.VMEM((subzones, zones * rows, LANES), f32),
+            pltpu.VMEM((subzones, zones * cap * 2 * SUBL, LANES), f32),
         ],
         compiler_params=room((8 * SWEEPS + 8) * seen.size + 2 * outgoing_size + (2 + subzones) * slot_size),
         name="solve",
@@ -365,8 +368,8 @@
         in_specs=[VMEM] * 8,
         out_specs=(VMEM, VMEM, VMEM),
         scratch_shapes=[
-            pltpu.VMEM((owned + 1, 2, *cells), f32),
-            pltpu.VMEM((owned + 1, 1, LANES), f32),
+            pltpu.VMEM((2, cap, owned + 1, 2, *cells), f32),
+            pltpu.VMEM((2, cap, owned + 1, 1, LANES), f32),
         ],
         compiler_params=room(10 * modulus.size + outgoing_size + 2 * slot_size),
         name="update",

time: 35.2 us -> 34.8 us (0.989)
    all_to_all x1, blocking collectives: 11.6 us -> 11.3 us  [on_device(): lax.all_to_all(slots, ('zone', 'line'), split_axis=0, concat_axis=0, tile...]
where the time goes in v6:
time: 34.8 us; the launch traced here: 34.5 us
  blocking collectives  11.3 us (32%)
  waiting for transfers between devices  8.89 us (26%)
  starting transfers between devices  7.37 us (21%)
  Pallas kernels  5.57 us (16%)
  between operations  1.37 us (4%)
    all_to_all x1, blocking collectives, on_device(): lax.all_to_all(slots, ('zone', 'line'), split_axis=0, concat_axis=0, tile...  11.3 us
    all_to_all x1, starting transfers between devices, on_device(): lax.all_to_all(outgoing, 'zone', split_axis=0, concat_axis=0, tiled=True)  7.29 us
    all_to_all x1, waiting for transfers between devices, on_device(): lax.all_to_all(outgoing, 'zone', split_axis=0, concat_axis=0, tiled=True)  6.3 us
    pallas_call x1, Pallas kernels, on_device(): pl.pallas_call(solve_kernel, out_shape=(half, half), in_specs=[VMEM, SMEM...  2.34 us
    pallas_call x1, Pallas kernels, on_device(): pl.pallas_call(pack_kernel, out_shape=(shape((zones * rows, LANES), f32),...  1.8 us
    ppermute x1, waiting for transfers between devices, on_device(): other = lax.ppermute(mine, 'core', other_core)  1.35 us
    ppermute x1, waiting for transfers between devices, on_device(): lax.ppermute(give, 'core', other_core)  1.24 us
    pallas_call x1, Pallas kernels, on_device(): pl.pallas_call(functools.partial(update_kernel, float(lines * cores)), ou...  0.99 us
  transfers between devices with their start and end apart: 3, of which 3 were waited for; matrix products, arithmetic and copies ran while one was open for 0% of the time, Pallas kernels for 1%

profile of v6, /device:TPU:0, one launch (start us, length us, event | category | flops | bytes accessed | tf_op | source)
XLA Modules:
  0.0 34.5 jit_solution(16759181587781081220)
XLA Ops:
  0.6 0.0 copy-start.1
  0.6 1.8 %pack.1 = (f32[272,128]{1,0:T(8,128)}, s32[2,8]{1,0:T(2,128)S(1)}, s32[8,8]{1,0:T(8,128)S(1)}) custom-call(s32[2,8]{1,0:T(2,128)} %bitcast.34, s32[4,8]{1,0:T(4,128)} %brick_hbm.1, f32[8,3,8,128]{3,2,1,0:T(8,128)} %bitcast.26, f32[8,8,128]{2,1,0:T(8,128)} %bitcast.29), custom_call_target="tpu_custom_call" | custom-call | tf_op jit(solution)/shard_map/pack/pallas_call | solution.py:299
  2.5 7.3 %all-to-all-start = ((f32[272,1,128]{2,1,0:T(1,128)}), f32[272,1,128]{2,1,0:T(1,128)S(1)}, u32[]{:S(2)}, u32[]{:S(2)}) async-start(f32[272,1,128]{2,1,0:T(1,128)} %bitcast.5), calls=%async_computation | async-start | bytes 278528 | tf_op jit(solution)/shard_map/all_to_all | solution.py:319
  10.4 0.0 copy-done.1
  10.4 0.4 %prepare.1 = (f32[8,8,8,128]{3,2,1,0:T(8,128)S(1)}, f32[8,8,8,128]{3,2,1,0:T(8,128)S(1)}, bf16[256,256]{1,0:T(8,128)(2,1)S(1)}) custom-call(f32[512,128]{1,0:T(8,128)S(1)} %bitcast.28), custom_call_target="tpu_custom_call" | custom-call | flops 16777216 | bytes 1048576 | tf_op jit(solution)/shard_map/prepare/pallas_call | solution.py:323
  10.8 6.3 %all-to-all-done = f32[272,1,128]{2,1,0:T(1,128)S(1)} async-done(((f32[272,1,128]{2,1,0:T(1,128)}), f32[272,1,128]{2,1,0:T(1,128)S(1)}, u32[]{:S(2)}, u32[]{:S(2)}) %all-to-all-start) | async-done | bytes 139296 | tf_op jit(solution)/shard_map/all_to_all | solution.py:319
  17.1 2.3 %solve.1 = (f32[8,2,8,128]{3,2,1,0:T(8,128)S(1)}, f32[8,2,8,128]{3,2,1,0:T(8,128)S(1)}) custom-call(s32[8,8]{1,0:T(8,128)S(1)} %get-tuple-element.15.brick_ref, f32[1]{0:T(128)S(6)} %copy.33.wave_ref, f32[272,128]{1,0:T(8,128)S(1)} %bitcast.22, f32[8,8,8,128]{3,2,1,0:T(8,128)S(1)} %get-tuple-element.17.start_ref, ...), custom_call_target="tpu_custom_call" | custom-call | tf_op jit(solution)/shard_map/solve/pallas_call | solution.py:334
  19.5 0.1 collective-permute-start
  19.6 1.2 %collective-permute-done.given_ref = f32[8,2,8,128]{3,2,1,0:T(8,128)S(1)} collective-permute-done((f32[8,2,8,128]{3,2,1,0:T(8,128)S(1)}, f32[8,2,8,128]{3,2,1,0:T(8,128)S(1)}, u32[]{:S(2)}, u32[]{:S(2)}) %collective-permute-start) | collective-permute-done | bytes 65568 | tf_op jit(solution)/shard_map/ppermute | solution.py:359
  20.8 0.0 copy-start.4
  20.8 0.0 copy-start
  20.8 0.0 copy-start.2
  20.8 0.0 copy-start.3
  20.9 11.3 %all_to_all.10 = f32[16,2,8,128]{3,2,1,0:T(8,128)S(1)} all-to-all(f32[16,2,8,128]{3,2,1,0:T(8,128)S(1)} %bitcast.24), channel_id=1, replica_groups=mesh['zone'=8,'line'=2,'core'=2] {'zone','line'}, dimensions={0} | all-to-all | bytes 262144 | tf_op jit(solution)/shard_map/all_to_all | solution.py:361
  32.1 0.0 collective-permute-start.1
  32.1 1.3 %collective-permute-done.1 = f32[16,2,8,128]{3,2,1,0:T(8,128)S(1)} collective-permute-done((f32[16,2,8,128]{3,2,1,0:T(8,128)S(1)}, f32[16,2,8,128]{3,2,1,0:T(8,128)S(1)}, u32[]{:S(2)}, u32[]{:S(2)}) %collective-permute-start.1) | collective-permute-done | bytes 131104 | tf_op jit(solution)/shard_map/ppermute | solution.py:362
  33.5 0.0 copy-done.4
  33.5 0.0 copy-done
  33.5 0.0 copy-done.2
  33.5 0.0 copy-done.3
  33.5 1.0 %update.1 = (f32[8,3,8,128]{3,2,1,0:T(8,128)}, f32[8,3,8,128]{3,2,1,0:T(8,128)}, f32[8,3,8,128]{3,2,1,0:T(8,128)}) custom-call(s32[2,8]{1,0:T(2,128)S(1)} %get-tuple-element.14.send_ref, f32[8,2,2,8,128]{4,3,2,1,0:T(8,128)S(1)} %bitcast.25, f32[8,2,2,8,128]{4,3,2,1,0:T(8,128)S(1)} %bitcast.31, f32[272,128]{1,0:T(8,128)S(1)} %bitcast.23, ...), custom_call_target="tpu_custom_call" | custom-call | tf_op jit(solution)/shard_map/update/pallas_call | solution.py:365
  (1 shorter events, 0.0 us)
Async XLA Ops:
  0.6 9.8 %copy-start.1 = (f32[1,4,2,8,1024]{4,3,2,1,0:T(8,128)S(1)}, f32[1,4,2,8,1024]{4,3,2,1,0:T(8,128)}, u32[]{:S(2)}) copy-start(f32[1,4,2,8,1024]{4,3,2,1,0:T(8,128)} %param.12) | copy-start | bytes 786436
  2.5 14.7 %all-to-all-start = ((f32[272,1,128]{2,1,0:T(1,128)}), f32[272,1,128]{2,1,0:T(1,128)S(1)}, u32[]{:S(2)}, u32[]{:S(2)}) async-start(f32[272,1,128]{2,1,0:T(1,128)} %bitcast.5), calls=%async_computation | async-start | bytes 278528 | tf_op jit(solution)/shard_map/all_to_all | solution.py:319
  19.5 1.3 %collective-permute-start = (f32[8,2,8,128]{3,2,1,0:T(8,128)S(1)}, f32[8,2,8,128]{3,2,1,0:T(8,128)S(1)}, u32[]{:S(2)}, u32[]{:S(2)}) collective-permute-start(f32[8,2,8,128]{3,2,1,0:T(8,128)S(1)} %get-tuple-element.21), channel_id=1, source_target_pairs={{0,1},{1,0},{2,3},{3,2},{4,5},{5,4},{6,7},{7,6},{8,9},{9,8},{10,11... | collective-permute-start | bytes 196616 | tf_op jit(solution)/shard_map/ppermute | solution.py:359
  20.8 12.7 %copy-start.4 = (f32[8,3,1,1024]{3,2,1,0:T(1,128)S(1)}, f32[8,3,1,1024]{3,2,1,0:T(1,128)}, u32[]{:S(2)}) copy-start(f32[8,3,1,1024]{3,2,1,0:T(1,128)} %param.10) | copy-start | bytes 294916
  20.8 12.7 %copy-start = (f32[8,3,1,1024]{3,2,1,0:T(1,128)S(1)}, f32[8,3,1,1024]{3,2,1,0:T(1,128)}, u32[]{:S(2)}) copy-start(f32[8,3,1,1024]{3,2,1,0:T(1,128)} %param.8) | copy-start | bytes 294916
  20.8 12.6 %copy-start.2 = (f32[8,1,1024]{2,1,0:T(1,128)S(1)}, f32[8,1,1024]{2,1,0:T(1,128)}, u32[]{:S(2)}) copy-start(f32[8,1,1024]{2,1,0:T(1,128)} %param.11) | copy-start | bytes 98308
  20.8 12.6 %copy-start.3 = (f32[8,3,1,1024]{3,2,1,0:T(1,128)S(1)}, f32[8,3,1,1024]{3,2,1,0:T(1,128)}, u32[]{:S(2)}) copy-start(f32[8,3,1,1024]{3,2,1,0:T(1,128)} %param.9) | copy-start | bytes 294916
  32.1 1.3 %collective-permute-start.1 = (f32[16,2,8,128]{3,2,1,0:T(8,128)S(1)}, f32[16,2,8,128]{3,2,1,0:T(8,128)S(1)}, u32[]{:S(2)}, u32[]{:S(2)}) collective-permute-start(f32[16,2,8,128]{3,2,1,0:T(8,128)S(1)} %all_to_all.10), channel_id=1, source_target_pairs={{0,1},{1,0},{2,3},{3,2},{4,5},{5,4},{6,7},{7,6},{8,9},{9,8},{10,11... | collective-permute-start | bytes 393224 | tf_op jit(solution)/shard_map/ppermute | solution.py:362

commit v7 on v6

--- a/solution.py
+++ b/solution.py
@@ -101,7 +101,7 @@
     return res
 
 
-def prepare_kernel(seen_ref, field_out, sten_out, table_out, res_ref):
+def prepare(seen_ref, field_out, sten_out, table_out, res_ref):
     source = lax.broadcasted_iota(jnp.int32, table_out.shape, 0) % LANES
     column = lax.broadcasted_iota(jnp.int32, table_out.shape, 1)
     target = column % LANES
@@ -126,17 +126,18 @@
 
 
 def solve_kernel(
-    brick_ref, wave_ref, data_ref, start_ref, sten0_ref, table_ref, keep_ref, give_ref,
-    coef_ref, field_ref, sten_ref, lam_ref, grad_ref, res_ref, sum_ref,
+    brick_ref, wave_ref, data_ref, seen_ref, keep_ref, give_ref,
+    start_ref, sten0_ref, table_ref, coef_ref, field_ref, sten_ref, lam_ref, grad_ref, res_ref, sum_ref,
 ):
     subzones, entries = brick_ref.shape[0] // 2, brick_ref.shape[1]
     rows = 2 * subzones
     zones, cap = keep_ref.shape[:2]
     core = lax.axis_index("core")
-    wave = wave_ref[0]
+    wave = jnp.broadcast_to(wave_ref[:, :1], (SUBL, LANES))
     table = brick_ref[...]
     starts = [[table[s, k] for k in range(entries)] for s in range(subzones)]
     slots = [[pl.multiple_of(table[subzones + s, k], SUBL) for k in range(entries)] for s in range(subzones)]
+    prepare(seen_ref, start_ref, sten0_ref, table_ref, res_ref)
     grid = [(x, y) for x in range(entries) for y in range(SUBL)]
 
     def swap(v):
@@ -315,28 +316,23 @@
         compiler_params=room(outgoing_size + 4 * modulus.size),
         name="pack",
     )(*(pltpu.with_memory_space_constraint(a, pltpu.HBM) for a in (send_list[0].T, brick_list, mod, fib)))
+    wave = lax.pad(wave_sq, f32(0), ((0, LANES - 1, 0),))[None]
+    outgoing, wave = lax.optimization_barrier((outgoing, wave))
     outgoing = outgoing.reshape(zones * rows, 1, LANES)
     arrived = lax.all_to_all(outgoing, "zone", split_axis=0, concat_axis=0, tiled=True).reshape(zones * rows, LANES)
     state = (K, SUBL, 2 * subzones, LANES)
     sites = K * SUBL * 2 * subzones
     table = (2 * LANES, 2 * LANES)
-    start, sten0, neighbours = pl.pallas_call(
-        prepare_kernel,
-        out_shape=(shape(state, f32), shape(state, f32), shape(table, jnp.bfloat16)),
-        in_specs=[VMEM],
-        out_specs=(VMEM,) * 3,
-        scratch_shapes=[pltpu.VMEM((sites, 2 * LANES), f32)],
-        compiler_params=room(8 * seen.size),
-        cost_estimate=pl.CostEstimate(flops=2**24, bytes_accessed=16 * seen.size, transcendentals=0),
-        name="prepare",
-    )(seen)
     half = shape((zones, cap, *cells), f32)
     keep, give = pl.pallas_call(
         solve_kernel,
         out_shape=(half, half),
-        in_specs=[VMEM, SMEM] + [VMEM] * 4,
+        in_specs=[VMEM] * 4,
         out_specs=(VMEM, VMEM),
         scratch_shapes=[
+            pltpu.VMEM(state, f32),
+            pltpu.VMEM(state, f32),
+            pltpu.VMEM(table, jnp.bfloat16),
             pltpu.VMEM((3, sites, LANES), f32),
             pltpu.VMEM((SWEEPS - 1, *state), f32),
             pltpu.VMEM((SWEEPS, 2, *state), f32),
@@ -345,9 +341,9 @@
             pltpu.VMEM((sites, 2 * LANES), f32),
             pltpu.VMEM((subzones, zones * cap * 2 * SUBL, LANES), f32),
         ],
-        compiler_params=room((8 * SWEEPS + 8) * seen.size + 2 * outgoing_size + (2 + subzones) * slot_size),
+        compiler_params=room((8 * SWEEPS + 11) * seen.size + 2 * outgoing_size + (2 + subzones) * slot_size),
         name="solve",
-    )(bricks, wave_sq, arrived, start, sten0, neighbours)
+    )(bricks, wave, arrived, seen)
     other_core = [(0, 1), (1, 0)]
     slots = pl.pallas_call(
         join_kernel,

time: 34.8 us -> 34.6 us (level)
  blocking collectives: 11.3 us -> 25.7 us
  starting transfers between devices: 7.37 us -> 0.07 us
  waiting for transfers between devices: 8.89 us -> 2.59 us
  Pallas kernels: 5.57 us -> 4.56 us
    all_to_all x0 -> x1, blocking collectives: none -> 14.5 us  [on_device(): lax.all_to_all(outgoing, 'zone', split_axis=0, concat_axis=0, tiled=True)]
    all_to_all x1 -> x0, starting transfers between devices: 7.29 us -> none  [on_device(): lax.all_to_all(outgoing, 'zone', split_axis=0, concat_axis=0, tiled=True)]
    all_to_all x1 -> x0, waiting for transfers between devices: 6.3 us -> none  [on_device(): lax.all_to_all(outgoing, 'zone', split_axis=0, concat_axis=0, tiled=True)]
    pallas_call x1, Pallas kernels: 1.8 us -> 1.12 us  [on_device(): pl.pallas_call(pack_kernel, out_shape=(shape((zones * rows, LANES), f32),...]
    pallas_call x2 -> x1, Pallas kernels: 2.77 us -> 2.45 us  [on_device(): pl.pallas_call(solve_kernel, out_shape=(half, half), in_specs=[VMEM] * 4,...]
  transfers between devices with their start and end apart: 3 -> 2, of which waited for: 3 -> 2; matrix products, arithmetic and copies ran while one was open for 0% -> 0% of each run, Pallas kernels for 1% -> 0%
where the time goes in v7:
time: 34.6 us; the launch traced here: 34.4 us
  blocking collectives  25.7 us (74%)
  Pallas kernels  4.56 us (13%)
  waiting for transfers between devices  2.59 us (7%)
  between operations  1.4 us (4%)
    all_to_all x1, blocking collectives, on_device(): lax.all_to_all(outgoing, 'zone', split_axis=0, concat_axis=0, tiled=True)  14.5 us
    all_to_all x1, blocking collectives, on_device(): lax.all_to_all(slots, ('zone', 'line'), split_axis=0, concat_axis=0, tile...  11.3 us
    pallas_call x1, Pallas kernels, on_device(): pl.pallas_call(solve_kernel, out_shape=(half, half), in_specs=[VMEM] * 4,...  2.45 us
    ppermute x1, waiting for transfers between devices, on_device(): other = lax.ppermute(mine, 'core', other_core)  1.35 us
    ppermute x1, waiting for transfers between devices, on_device(): lax.ppermute(give, 'core', other_core)  1.24 us
    pallas_call x1, Pallas kernels, on_device(): pl.pallas_call(pack_kernel, out_shape=(shape((zones * rows, LANES), f32),...  1.12 us
    pallas_call x1, Pallas kernels, on_device(): pl.pallas_call(functools.partial(update_kernel, float(lines * cores)), ou...  0.98 us
  transfers between devices with their start and end apart: 2, of which 2 were waited for; matrix products, arithmetic and copies ran while one was open for 0% of the time, Pallas kernels for 0%

profile of v7, /device:TPU:0, one launch (start us, length us, event | category | flops | bytes accessed | tf_op | source)
XLA Modules:
  0.0 34.4 jit_solution(12934731810241981988)
XLA Ops:
  0.6 0.0 copy-start.1
  1.3 1.1 %pack.1 = (f32[272,128]{1,0:T(8,128)S(1)}, s32[2,8]{1,0:T(2,128)S(1)}, s32[8,8]{1,0:T(8,128)S(1)}) custom-call(s32[2,8]{1,0:T(2,128)} %bitcast.37, s32[4,8]{1,0:T(4,128)} %brick_hbm.1, f32[8,3,8,128]{3,2,1,0:T(8,128)} %bitcast.28, f32[8,8,128]{2,1,0:T(8,128)} %bitcast.32), custom_call_target="tpu_custom_call" | custom-call | tf_op jit(solution)/shard_map/pack/pallas_call | solution.py:300
  2.5 14.5 %all_to_all.10 = f32[272,1,128]{2,1,0:T(1,128)S(1)} all-to-all(f32[272,1,128]{2,1,0:T(1,128)S(1)} %bitcast.31), channel_id=1, replica_groups=mesh['zone'=8,'line'=2,'core'=2] {'zone'}, dimensions={0} | all-to-all | bytes 278528 | tf_op jit(solution)/shard_map/all_to_all | solution.py:322
  16.9 0.0 copy-done.1
  16.9 2.4 %solve.1 = (f32[8,2,8,128]{3,2,1,0:T(8,128)S(1)}, f32[8,2,8,128]{3,2,1,0:T(8,128)S(1)}) custom-call(s32[8,8]{1,0:T(8,128)S(1)} %get-tuple-element.14.brick_ref, f32[1,128]{1,0:T(1,128)S(1)} %pad_bitcast_fusion.wave_ref, f32[272,128]{1,0:T(8,128)S(1)} %bitcast.24, f32[512,128]{1,0:T(8,128)S(1)} %bitcast.30), custom_call_target="tpu_custom_call" | custom-call | tf_op jit(solution)/shard_map/solve/pallas_call | solution.py:327
  19.4 0.1 collective-permute-start
  19.5 1.2 %collective-permute-done.given_ref = f32[8,2,8,128]{3,2,1,0:T(8,128)S(1)} collective-permute-done((f32[8,2,8,128]{3,2,1,0:T(8,128)S(1)}, f32[8,2,8,128]{3,2,1,0:T(8,128)S(1)}, u32[]{:S(2)}, u32[]{:S(2)}) %collective-permute-start) | collective-permute-done | bytes 65568 | tf_op jit(solution)/shard_map/ppermute | solution.py:355
  20.7 0.0 copy-start.4
  20.7 0.0 copy-start
  20.7 0.0 copy-start.2
  20.8 0.0 copy-start.3
  20.8 11.3 %all_to_all.11 = f32[16,2,8,128]{3,2,1,0:T(8,128)S(1)} all-to-all(f32[16,2,8,128]{3,2,1,0:T(8,128)S(1)} %bitcast.26), channel_id=1, replica_groups=mesh['zone'=8,'line'=2,'core'=2] {'zone','line'}, dimensions={0} | all-to-all | bytes 262144 | tf_op jit(solution)/shard_map/all_to_all | solution.py:357
  32.0 0.0 collective-permute-start.1
  32.0 1.3 %collective-permute-done.1 = f32[16,2,8,128]{3,2,1,0:T(8,128)S(1)} collective-permute-done((f32[16,2,8,128]{3,2,1,0:T(8,128)S(1)}, f32[16,2,8,128]{3,2,1,0:T(8,128)S(1)}, u32[]{:S(2)}, u32[]{:S(2)}) %collective-permute-start.1) | collective-permute-done | bytes 131104 | tf_op jit(solution)/shard_map/ppermute | solution.py:358
  33.4 0.0 copy-done.4
  33.4 0.0 copy-done
  33.4 0.0 copy-done.2
  33.4 0.0 copy-done.3
  33.4 1.0 %update.1 = (f32[8,3,8,128]{3,2,1,0:T(8,128)}, f32[8,3,8,128]{3,2,1,0:T(8,128)}, f32[8,3,8,128]{3,2,1,0:T(8,128)}) custom-call(s32[2,8]{1,0:T(2,128)S(1)} %get-tuple-element.13.send_ref, f32[8,2,2,8,128]{4,3,2,1,0:T(8,128)S(1)} %bitcast.27, f32[8,2,2,8,128]{4,3,2,1,0:T(8,128)S(1)} %bitcast.34, f32[272,128]{1,0:T(8,128)S(1)} %bitcast.25, ...), custom_call_target="tpu_custom_call" | custom-call | tf_op jit(solution)/shard_map/update/pallas_call | solution.py:361
  (2 shorter events, 0.0 us)
Async XLA Ops:
  0.6 16.3 %copy-start.1 = (f32[1,4,2,8,1024]{4,3,2,1,0:T(8,128)S(1)}, f32[1,4,2,8,1024]{4,3,2,1,0:T(8,128)}, u32[]{:S(2)}) copy-start(f32[1,4,2,8,1024]{4,3,2,1,0:T(8,128)} %param.12) | copy-start | bytes 786436
  19.4 1.3 %collective-permute-start = (f32[8,2,8,128]{3,2,1,0:T(8,128)S(1)}, f32[8,2,8,128]{3,2,1,0:T(8,128)S(1)}, u32[]{:S(2)}, u32[]{:S(2)}) collective-permute-start(f32[8,2,8,128]{3,2,1,0:T(8,128)S(1)} %get-tuple-element.19), channel_id=1, source_target_pairs={{0,1},{1,0},{2,3},{3,2},{4,5},{5,4},{6,7},{7,6},{8,9},{9,8},{10,11... | collective-permute-start | bytes 196616 | tf_op jit(solution)/shard_map/ppermute | solution.py:355
  20.7 12.7 %copy-start.4 = (f32[8,3,1,1024]{3,2,1,0:T(1,128)S(1)}, f32[8,3,1,1024]{3,2,1,0:T(1,128)}, u32[]{:S(2)}) copy-start(f32[8,3,1,1024]{3,2,1,0:T(1,128)} %param.10) | copy-start | bytes 294916
  20.7 12.7 %copy-start = (f32[8,3,1,1024]{3,2,1,0:T(1,128)S(1)}, f32[8,3,1,1024]{3,2,1,0:T(1,128)}, u32[]{:S(2)}) copy-start(f32[8,3,1,1024]{3,2,1,0:T(1,128)} %param.8) | copy-start | bytes 294916
  20.7 12.6 %copy-start.2 = (f32[8,1,1024]{2,1,0:T(1,128)S(1)}, f32[8,1,1024]{2,1,0:T(1,128)}, u32[]{:S(2)}) copy-start(f32[8,1,1024]{2,1,0:T(1,128)} %param.11) | copy-start | bytes 98308
  20.8 12.6 %copy-start.3 = (f32[8,3,1,1024]{3,2,1,0:T(1,128)S(1)}, f32[8,3,1,1024]{3,2,1,0:T(1,128)}, u32[]{:S(2)}) copy-start(f32[8,3,1,1024]{3,2,1,0:T(1,128)} %param.9) | copy-start | bytes 294916
  32.0 1.3 %collective-permute-start.1 = (f32[16,2,8,128]{3,2,1,0:T(8,128)S(1)}, f32[16,2,8,128]{3,2,1,0:T(8,128)S(1)}, u32[]{:S(2)}, u32[]{:S(2)}) collective-permute-start(f32[16,2,8,128]{3,2,1,0:T(8,128)S(1)} %all_to_all.11), channel_id=1, source_target_pairs={{0,1},{1,0},{2,3},{3,2},{4,5},{5,4},{6,7},{7,6},{8,9},{9,8},{10,11... | collective-permute-start | bytes 393224 | tf_op jit(solution)/shard_map/ppermute | solution.py:358
